TPU v7x, 32 devices: a 4x4x1 block of a 4x4x8 slice. The times are simulated.
32 devices in a mesh: dp: 1 (over z), ep: 32 (over y, x, core).
Axes of the slice: x: 4, y: 4, z: 1, core: 2. Of those that a mesh axis runs over, the one named last changes fastest.
The devices are a block of a 4x4x8 slice.
Arguments:
- tokens: bfloat16 [2048, 2048], P(('dp', 'ep'))
- routes: int32 [2048, 8], P(('dp', 'ep'))
- w_router: bfloat16 [2048, 128], replicated
- w_one: bfloat16 [128, 2048, 768], P('ep')
- w_three: bfloat16 [128, 2048, 768], P('ep')
- w_two: bfloat16 [128, 768, 2048], P('ep')
Outputs:
- output: bfloat16 [2048, 2048], P(('dp', 'ep'))
All inputs are finite; a program needn't handle non-finite values.
Results may differ from a plain program's by a relative error of at most 0.00819039.
Values are sent between devices in bfloat16 or wider.
A program may use at most 768 MiB of HBM per device.

v0:
```python
import jax
import jax.numpy as jnp
from jax import lax
from jax.sharding import PartitionSpec as P


def slot_capacity(num_tokens, top_k, num_experts):
    return 8 * ((3 * num_tokens * top_k + 16 * num_experts - 1) // (16 * num_experts))


def route_gates(tokens, routes, w_router):
    logits = jnp.dot(tokens, w_router, preferred_element_type=jnp.float32)
    return jax.nn.softmax(jnp.take_along_axis(logits, routes, axis=1), axis=-1)


def dispatch_plan(routes, num_experts, capacity):
    top_k = routes.shape[1]
    flat_routes = routes.reshape(-1)
    num_pairs = flat_routes.shape[0]
    sort_order = jnp.argsort(flat_routes, stable=True)
    counts = jax.ops.segment_sum(jnp.ones_like(flat_routes), flat_routes, num_segments=num_experts)
    starts = jnp.cumsum(counts) - counts
    slot_ids = starts[:, None] + jnp.arange(capacity, dtype=jnp.int32)[None, :]
    token_at = sort_order[jnp.minimum(slot_ids, num_pairs - 1)] // top_k
    pair_rank = jnp.zeros_like(sort_order).at[sort_order].set(jnp.arange(num_pairs, dtype=sort_order.dtype))
    pair_row = flat_routes * capacity + pair_rank - starts[flat_routes]
    return token_at, pair_row


def expert_mlp(rows, w_one, w_three, w_two):
    gate_pre = jnp.einsum('erd,edf->erf', rows, w_one, preferred_element_type=jnp.float32)
    up_pre = jnp.einsum('erd,edf->erf', rows, w_three, preferred_element_type=jnp.float32)
    hidden = (jax.nn.silu(gate_pre) * up_pre).astype(jnp.bfloat16)
    return jnp.einsum('erf,efd->erd', hidden, w_two, preferred_element_type=jnp.float32).astype(jnp.bfloat16)


def solution(mesh):
    group_size = mesh.shape['ep']
    row_spec = P(('dp', 'ep'), None)
    expert_spec = P('ep', None, None)

    def device_step(tokens, routes, w_router, w_one, w_three, w_two):
        num_tokens, d_model = tokens.shape
        top_k = routes.shape[1]
        num_experts = w_router.shape[1]
        local_experts = w_one.shape[0]
        capacity = slot_capacity(num_tokens, top_k, num_experts)
        gate_vals = route_gates(tokens, routes, w_router)
        token_at, pair_row = dispatch_plan(routes, num_experts, capacity)
        send_rows = tokens[token_at].reshape(num_experts, 1, capacity, d_model)
        recv_rows = lax.all_to_all(send_rows, 'ep', 0, 1, tiled=True)
        out_rows = expert_mlp(recv_rows.reshape(local_experts, group_size * capacity, d_model), w_one, w_three, w_two)
        back_rows = lax.all_to_all(out_rows.reshape(local_experts, group_size, capacity, d_model), 'ep', 1, 0, tiled=True)
        pair_out = back_rows.reshape(num_experts * capacity, d_model)[pair_row].reshape(num_tokens, top_k, d_model)
        return jnp.sum(gate_vals[:, :, None] * pair_out, axis=1).astype(jnp.bfloat16)

    return jax.shard_map(device_step, mesh=mesh, in_specs=(row_spec, row_spec, P(None, None), expert_spec, expert_spec, expert_spec), out_specs=row_spec, check_vma=False)
```

profile of v0, /device:TPU:103, one launch (start us, length us, event | category | flops | bytes accessed | tf_op | source)
XLA Modules:
  0.0 187.8 jit_solution(14954533981819829327)
XLA Ops:
  0.0 0.8 copy.34
  0.9 3.8 %sort.17 = (s32[512]{0:T(512)}, s32[512]{0:T(512)S(1)}) sort(s32[512]{0:T(512)S(1)} %reshape.205, s32[512]{0:T(512)S(1)} %iota.13), dimensions={0}, to_apply=%region_2.3 | sort | flops 4608 | bytes 8192 | tf_op jit(solution)/shard_map/jit(argsort)/sort | solution.py:20
  4.7 4.1 %scatter_custom_fusion = s32[128]{0:T(128)S(1)} fusion(s32[512]{0:T(512)S(1)} %reshape.205, s32[512]{0:T(512)S(1)} %broadcast.168, s32[]{:T(128)} %constant.17.clone.1), kind=kCustom, calls=%fused_computation.42 | custom fusion | flops 512 | bytes 516 | tf_op jit(solution)/shard_map/scatter-add | solution.py:21
  8.8 0.1 copy.35
  8.9 0.2 reduce-window.9
  9.1 0.1 reduce
  9.2 0.1 compare_select_fusion.1
  9.4 6.9 %gather_fusion = s32[1024]{0:T(1024)S(1)} fusion(s32[512]{0:T(512)S(1)} %get-tuple-element.6, s32[1024]{0:T(1024)S(1)} %broadcast_clamp_fusion.1), kind=kCustom, calls=%fused_computation | custom fusion | bytes 12288 | tf_op jit(solution)/shard_map/gather | solution.py:24
  16.5 0.7 copy-done.1
  17.2 6.0 %gather_fusion.1 = bf16[1024,2048]{1,0:T(8,128)(2,1)} fusion(bf16[64,2048]{1,0:T(8,128)(2,1)S(1)} %copy-done.1, s32[1024]{0:T(1024)S(1)} %broadcast_clamp_fusion), kind=kCustom, calls=%fused_computation.1 | custom fusion | bytes 8392704 | tf_op jit(solution)/shard_map/gather | solution.py:50
  23.2 59.6 %all_to_all.30 = bf16[128,1,8,2048]{3,2,1,0:T(8,128)(2,1)S(1)} all-to-all(bf16[128,1,8,2048]{3,2,1,0:T(8,128)(2,1)} %bitcast.41), channel_id=1, replica_groups=mesh['dp'=1,'ep'=32] {'ep'}, dimensions={0} | all-to-all | bytes 8388608 | tf_op jit(solution)/shard_map/all_to_all | solution.py:51
  82.8 2.0 %copy-done.2 = bf16[128,1,8,2048]{3,2,1,0:T(8,128)(2,1)} copy-done((bf16[128,1,8,2048]{3,2,1,0:T(8,128)(2,1)}, bf16[128,1,8,2048]{3,2,1,0:T(8,128)(2,1)S(1)}, u32[]{:S(2)}) %copy-start.2) | copy-done | bytes 4194328
  84.8 9.7 %fusion.3 = f32[4,256,768]{2,1,0:T(8,128)} fusion(bf16[4,2048,768]{2,1,0:T(8,128)(2,1)} %param.9, bf16[4,32,1,8,2048]{4,3,0,1,2:T(8,128)(2,1)S(1)} %bitcast.42), kind=kOutput, calls=%fused_computation.11 | convolution fusion | flops 3221225472 | bytes 19922944 | tf_op jit(solution)/shard_map/erd,edf->erf/dot_general | solution.py:31
  94.5 15.3 %convert_bitcast_fusion = bf16[4,32,8,2048]{3,2,1,0:T(8,128)(2,1)} fusion(bf16[4,768,2048]{2,1,0:T(8,128)(2,1)} %param.11, f32[4,256,768]{2,1,0:T(8,128)} %fusion.3, bf16[4,2048,768]{2,1,0:T(8,128)(2,1)} %param.10, bf16[4,32,1,8,2048]{4,3,0,1,2:T(8,128)(2,1)} %bitcast.43), kind=kOutput, calls=%fused_computation.13 | convolution fusion | flops 6449266688 | bytes 36700160 | tf_op jit(solution)/shard_map/erf,efd->erd/dot_general | solution.py:34
  109.9 4.7 %copy.38 = bf16[4,32,8,2048]{3,2,0,1:T(8,128)(2,1)} copy(bf16[4,32,8,2048]{3,2,1,0:T(8,128)(2,1)} %convert_bitcast_fusion) | data formatting | bytes 8388608 | tf_op jit(solution)/shard_map/reshape | solution.py:53
  114.6 6.9 %all-to-all-start.1 = ((bf16[4,32,8,2048]{3,2,0,1:T(8,128)(2,1)}), bf16[4,32,8,2048]{3,2,0,1:T(8,128)(2,1)}, u32[]{:S(2)}, u32[]{:S(2)}) async-start(bf16[4,32,8,2048]{3,2,0,1:T(8,128)(2,1)} %copy.38), calls=%async_computation.1 | async-start | bytes 8388608 | tf_op jit(solution)/shard_map/all_to_all | solution.py:53
  121.7 0.1 reshape.245
  121.8 0.2 fusion.22
  122.1 3.6 %gather_fusion.4 = f32[512]{0:T(512)S(1)} fusion(f32[64,128]{1,0:T(8,128)S(1)} %fusion.22, s32[512]{0:T(512)S(1)} %reshape.245), kind=kCustom, calls=%fused_computation.4 | custom fusion | bytes 8192 | tf_op jit(solution)/shard_map/jit(take_along_axis)/gather | solution.py:13
  126.0 3.3 %gather_fusion.2 = s32[512]{0:T(512)S(1)} fusion(s32[128]{0:T(128)S(1)} %sub.24, s32[1024]{0:T(1024)S(1)} %pad_clamp_fusion.1), kind=kCustom, calls=%fused_computation.2 | custom fusion | bytes 6144 | tf_op jit(solution)/shard_map/gather | solution.py:26
  129.4 2.6 %scatter_custom_fusion.1 = s32[512]{0:T(512)S(1)} fusion(s32[512]{0:T(512)S(1)} %compare_select_fusion.5, s32[512]{0:T(512)S(1)} %iota.14, s32[]{:T(128)} %constant.17.clone.1), kind=kCustom, calls=%fused_computation.40 | custom fusion | bytes 2052 | tf_op jit(solution)/shard_map/scatter | solution.py:25
  132.1 46.1 %all-to-all-done.1 = bf16[4,32,8,2048]{3,2,0,1:T(8,128)(2,1)} async-done(((bf16[4,32,8,2048]{3,2,0,1:T(8,128)(2,1)}), bf16[4,32,8,2048]{3,2,0,1:T(8,128)(2,1)}, u32[]{:S(2)}, u32[]{:S(2)}) %all-to-all-start.1) | async-done | bytes 4194336 | tf_op jit(solution)/shard_map/all_to_all | solution.py:53
  178.1 7.1 %gather_fusion.3 = bf16[512,2048]{1,0:T(8,128)(2,1)S(1)} fusion(bf16[1024,2048]{1,0:T(8,128)(2,1)} %bitcast.10, s32[1024]{0:T(1024)S(1)} %pad_clamp_fusion), kind=kCustom, calls=%fused_computation.3 | custom fusion | bytes 4196352 | tf_op jit(solution)/shard_map/gather | solution.py:54
  185.3 2.5 %fusion = bf16[64,2048]{1,0:T(8,128)(2,1)} fusion(bf16[512,2048]{1,0:T(8,128)(2,1)S(1)} %gather_fusion.3, f32[64,8]{1,0:T(8,128)S(1)} %copy.33), kind=kLoop, calls=%fused_computation.8 | loop fusion | flops 3014656 | bytes 2361344 | tf_op jit(solution)/shard_map/reduce_sum | solution.py:55
  (31 shorter events, 0.9 us)
Async XLA Ops:
  0.0 121.8 %copy-start = (bf16[2048,128]{1,0:T(8,128)(2,1)S(1)}, bf16[2048,128]{1,0:T(8,128)(2,1)}, u32[]{:S(2)}) copy-start(bf16[2048,128]{1,0:T(8,128)(2,1)} %param.8) | copy-start | bytes 1572868
  16.3 1.0 copy-start.1
  82.8 2.0 %copy-start.2 = (bf16[128,1,8,2048]{3,2,1,0:T(8,128)(2,1)}, bf16[128,1,8,2048]{3,2,1,0:T(8,128)(2,1)S(1)}, u32[]{:S(2)}) copy-start(bf16[128,1,8,2048]{3,2,1,0:T(8,128)(2,1)S(1)} %all_to_all.30) | copy-start | bytes 12582916
  114.6 7.0 %copy-start.3 = (s32[64,8]{0,1:T(8,128)S(1)}, s32[64,8]{0,1:T(8,128)}, u32[]{:S(2)}) copy-start(s32[64,8]{0,1:T(8,128)} %param.7) | copy-start | bytes 6148
  114.6 63.5 %all-to-all-start.1 = ((bf16[4,32,8,2048]{3,2,0,1:T(8,128)(2,1)}), bf16[4,32,8,2048]{3,2,0,1:T(8,128)(2,1)}, u32[]{:S(2)}, u32[]{:S(2)}) async-start(bf16[4,32,8,2048]{3,2,0,1:T(8,128)(2,1)} %copy.38), calls=%async_computation.1 | async-start | bytes 8388608 | tf_op jit(solution)/shard_map/all_to_all | solution.py:53
where the time goes:
time: 188 us
  blocking collectives  59.6 us (32%)
  waiting for transfers between devices  46.1 us (25%)
  local copies, waits for them, and re-layouts  38.8 us (21%)
  matrix products  25.3 us (13%)
  other arithmetic  10.9 us (6%)
  starting transfers between devices  6.91 us (4%)
    all_to_all x1, blocking collectives, device_step(): recv_rows = lax.all_to_all(send_rows, 'ep', 0, 1, tiled=True)  59.6 us
    all_to_all x1, waiting for transfers between devices, device_step(): lax.all_to_all(out_rows.reshape(local_experts, group_size, capacity, d_mo...  46.1 us
    dot_general x1, matrix products, expert_mlp(): jnp.einsum('erf,efd->erd', hidden, w_two, preferred_element_type=jnp.floa...  15.3 us
    dot_general x1, matrix products, expert_mlp(): jnp.einsum('erd,edf->erf', rows, w_one, preferred_element_type=jnp.float32)  9.74 us
    gather x1, local copies, waits for them, and re-layouts, device_step(): back_rows.reshape(num_experts * capacity, d_model)[pair_row]  7.13 us
    gather x2, local copies, waits for them, and re-layouts, dispatch_plan(): token_at = sort_order[jnp.minimum(slot_ids, num_pairs - 1)] // top_k  6.95 us
    all_to_all x1, starting transfers between devices, device_step(): lax.all_to_all(out_rows.reshape(local_experts, group_size, capacity, d_mo...  6.91 us
    gather x1, local copies, waits for them, and re-layouts, device_step(): send_rows = tokens[token_at].reshape(num_experts, 1, capacity, d_model)  6.01 us
  transfers between devices with their start and end apart: 1, of which 1 were waited for; matrix products, arithmetic and copies ran while one was open for 6% of the time, Pallas kernels for 0%

commit v1 on v0

v1 whole, which is shorter than its diff:
```python
import functools
import math

import jax
import jax.numpy as jnp
from jax import lax
from jax.experimental import pallas as pl
from jax.experimental.pallas import tpu as pltpu
from jax.sharding import PartitionSpec as P

MESH = pl.DeviceIdType.MESH
F32 = jnp.float32
BF16 = jnp.bfloat16
CORES = 2
LANES = 128


def slot_capacity(num_tokens, top_k, num_experts):
    return 8 * ((3 * num_tokens * top_k + 16 * num_experts - 1) // (16 * num_experts))


def moe_kernel(
    side,
    x_hbm, routes_ref, wr_hbm, w1_hbm, w3_hbm, w2_hbm, y_ref,
    xg, wr, w1, w3, w2, xo, hid, meta, slots, gates, mbuf, pbuf, ybuf,
    x_sem, wr_sem, w_sem, meta_ssem, meta_rsem, first_ssem, second_ssem, relay_ssem, core_ssem, ag_rsem, r1_ssem, r1_rsem, r2_ssem, r2_rsem,
):
    num_devices = CORES * side * side
    chips = side * side
    num_tokens, d_model = x_hbm.shape
    half = d_model // 2
    quarter = half // CORES
    local_experts = w1.shape[0]
    d_expert = w1.shape[2]
    chip_experts = CORES * local_experts
    num_experts = num_devices * local_experts
    top_k = routes_ref.shape[0]
    cap = xo.shape[3] // CORES

    me = lax.axis_index('ep')
    core = lax.rem(me, CORES)
    my_x = lax.rem(lax.div(me, CORES), side)
    my_y = lax.div(me, CORES * side)

    def ring(v, k):
        return lax.rem(v + k, side)

    def chip_at(y, x):
        return y * side + x

    def dev(y, x, c):
        return chip_at(y, x) * CORES + c

    partner = dev(my_y, my_x, 1 - core)

    def remote(src, dst, ssem, rsem, target):
        return pltpu.make_async_remote_copy(src_ref=src, dst_ref=dst, send_sem=ssem, recv_sem=rsem, device_id={'ep': target}, device_id_type=MESH)

    x_copies = [pltpu.make_async_copy(x_hbm.at[:, pl.ds(h * half, half)], xg.at[h, me], x_sem.at[h]) for h in range(2)]
    for cp in x_copies:
        cp.start()
    wr_copy = pltpu.make_async_copy(wr_hbm, wr, wr_sem.at[0])
    wr_copy.start()

    def weight_copies(e):
        return [pltpu.make_async_copy(src.at[e], dst.at[e], w_sem.at[i, e]) for i, (src, dst) in enumerate(((w1_hbm, w1), (w3_hbm, w3), (w2_hbm, w2)))]

    def start_weights(e, carry):
        for cp in weight_copies(e):
            cp.start()
        return carry

    lax.fori_loop(0, local_experts, start_weights, 0)

    barrier = pltpu.get_barrier_semaphore()

    def greet(i, carry):
        pl.semaphore_signal(barrier, inc=1, device_id={'ep': lax.rem(me + i, num_devices)}, device_id_type=MESH)
        return carry

    lax.fori_loop(1, num_devices, greet, 0)
    pl.semaphore_wait(barrier, num_devices - 1)
    for cp in x_copies:
        cp.wait()

    def place(h, a, b):
        if h == 0:
            return ring(my_y, b), ring(my_x, a)
        return ring(my_y, a), ring(my_x, b)

    def block_src(h, a, b, c):
        y, x = place(h, a, b)
        return dev(y, x, c)

    def move_block(h, src, ssem, target):
        return remote(xg.at[h, src], xg.at[h, src], ssem, ag_rsem.at[h, src], target)

    def wait_block(h, src):
        pltpu.make_async_copy(xg.at[h, src], xg.at[h, src], ag_rsem.at[h, src]).wait()

    def first_copy(h, k):
        return move_block(h, me, first_ssem.at[h, k], block_src(h, k, 0, core))

    def second_copy(h, a, k):
        return move_block(h, block_src(h, a, 0, core), second_ssem.at[h, a, k], block_src(h, 0, k, core))

    def relay_copy(h, a, k):
        return move_block(h, block_src(h, a, k, core), relay_ssem.at[h, a], block_src(h, 0, side - k, core))

    def core_copy(h, a, b):
        return move_block(h, block_src(h, a, b, core), core_ssem.at[h, a, b], partner)

    for h in range(2):
        for k in (1, side - 1) + tuple(range(2, side - 1)):
            first_copy(h, k).start()
        for k in (1, side - 1):
            second_copy(h, 0, k).start()
        core_copy(h, 0, 0).start()

    wr_copy.wait()
    x_local = [xg[h, me] for h in range(2)]
    logits = sum(
        lax.dot_general(wr[pl.ds(h * half, half), :], x_local[h], (((0,), (1,)), ((), ())), preferred_element_type=F32)
        for h in range(2)
    )
    routes = routes_ref[...]
    expert_iota = lax.broadcasted_iota(jnp.int32, (num_experts, num_tokens), 0)
    picked = jnp.concatenate(
        [jnp.sum(jnp.where(expert_iota == routes[j:j + 1, :], logits, 0.0), axis=0, keepdims=True) for j in range(top_k)], axis=0)
    ex = jnp.exp(picked - jnp.max(picked, axis=0, keepdims=True))
    gate = ex / jnp.sum(ex, axis=0, keepdims=True)
    tile = jnp.concatenate([routes.astype(F32) + 1.0, gate], axis=0)
    lane = lax.broadcasted_iota(jnp.int32, (2 * top_k, LANES), 1)
    meta[me] = jnp.where(lane // num_tokens == core, jnp.concatenate([tile] * CORES, axis=1), 0.0)

    def meta_copy(i):
        return remote(meta.at[me], meta.at[me], meta_ssem.at[i], meta_rsem.at[me], lax.rem(me + i, num_devices))

    def send_meta(i, carry):
        meta_copy(i).start()
        return carry

    def recv_meta(i, carry):
        src = lax.rem(me + i, num_devices)
        pltpu.make_async_copy(meta.at[src], meta.at[src], meta_rsem.at[src]).wait()
        return carry

    def sent_meta(i, carry):
        meta_copy(i).wait_send()
        return carry

    lax.fori_loop(1, num_devices, send_meta, 0)
    lax.fori_loop(1, num_devices, recv_meta, 0)

    row_i = lax.broadcasted_iota(jnp.int32, (LANES, LANES), 0)
    col_i = lax.broadcasted_iota(jnp.int32, (LANES, LANES), 1)
    before = jnp.where((row_i < col_i) & (row_i // num_tokens == col_i // num_tokens), 1.0, 0.0).astype(BF16)
    ids = lax.broadcasted_iota(jnp.int32, (num_experts, LANES), 0).astype(F32) + 1.0

    def plan_chip(p, carry):
        both = meta[CORES * p] + meta[CORES * p + 1]
        mask = jnp.zeros((num_experts, LANES), F32)
        weight = jnp.zeros((num_experts, LANES), F32)
        for j in range(top_k):
            hit = ids == both[j:j + 1, :]
            mask = jnp.where(hit, 1.0, mask)
            weight = jnp.where(hit, both[top_k + j:top_k + j + 1, :], weight)
        rank = jnp.dot(mask.astype(BF16), before, preferred_element_type=F32)
        slots[p] = jnp.where(mask > 0.0, rank, -1.0)
        gates[p] = weight
        return carry

    lax.fori_loop(0, chips, plan_chip, 0)

    pair_row = lax.broadcasted_iota(jnp.int32, (CORES * cap, LANES), 0)
    pair_lane = lax.broadcasted_iota(jnp.int32, (CORES * cap, LANES), 1)
    wanted = jnp.where(pair_row // cap == pair_lane // num_tokens, pair_row % cap, -2).astype(F32)

    def gather_chip(h, y, x):
        p = chip_at(y, x)
        mine = slots[p, pl.ds(me * local_experts, local_experts), :]
        pick = jnp.where(mine[:, None, :] == wanted[None], 1.0, 0.0).reshape(local_experts * CORES * cap, LANES).astype(BF16)
        rows = xg[h, pl.ds(p * CORES, CORES)].reshape(CORES * num_tokens, half)
        out = jnp.dot(pick, rows, preferred_element_type=F32).astype(BF16)
        xo[:, y, x, :, pl.ds(h * half, half)] = out.reshape(local_experts, CORES * cap, half)

    def finish(a, b):
        for h in range(2):
            wait_block(h, block_src(h, a, b, 1 - core))
            gather_chip(h, *place(h, a, b))

    def land(h, a, b):
        wait_block(h, block_src(h, a, b, core))
        core_copy(h, a, b).start()

    far = side // 2
    near = (1, side - 1) + tuple(range(2, side - 1))

    def same_line(a, carry):
        for h in range(2):
            land(h, a, 0)
            for k in (1, side - 1):
                second_copy(h, a, k).start()
        return carry

    def next_lines(a, carry):
        for h in range(2):
            land(h, a, 1)
            relay_copy(h, a, 1).start()
            land(h, a + far, side - 1)
            relay_copy(h, a + far, side - 1).start()
            land(h, a + far, 1)
            land(h, a, side - 1)
        finish(a, 0)
        finish(a + far, 0)
        return carry

    def far_line(a, carry):
        for h in range(2):
            land(h, a, far)
        finish(a, 1)
        finish(a, side - 1)
        return carry

    def last_blocks(a, carry):
        finish(a, far)
        return carry

    lax.fori_loop(1, side, same_line, 0)
    lax.fori_loop(0, far, next_lines, 0)
    lax.fori_loop(0, side, far_line, 0)
    lax.fori_loop(0, side, last_blocks, 0)

    def r1_place(h, k):
        if h == 0:
            return ring(my_y, k), my_x
        return my_y, ring(my_x, k)

    def r1_src(h, e, k, cm):
        y, x = r1_place(h, k)
        cols = pl.ds(h * half + cm * quarter, quarter)
        if h == 0:
            return xo.at[e, y, :, :, cols]
        return xo.at[e, :, x, :, cols]

    def r1_copy(h, e, k, cm):
        y, x = r1_place(h, k)
        return remote(r1_src(h, e, k, cm), mbuf.at[h, k, core, e], r1_ssem.at[h, k, cm, e], r1_rsem.at[h, k, core, e], dev(y, x, cm))

    def r1_partner(h, e):
        y, x = my_y, my_x
        cols = pl.ds(pl.multiple_of(h * half + (1 - core) * quarter, quarter), quarter)
        src = xo.at[e, y, :, :, cols] if h == 0 else xo.at[e, :, x, :, cols]
        return remote(src, mbuf.at[h, 0, core, e], r1_ssem.at[h, 0, 0, e], r1_rsem.at[h, 0, core, e], partner)

    n1 = 256
    n2 = 512

    def expert(e, carry):
        copies = weight_copies(e)
        copies[0].wait()
        copies[1].wait()

        def up(t, c2):
            rows = xo[e].reshape(chips * CORES * cap, d_model)
            cols = pl.ds(pl.multiple_of(t * n1, n1), n1)
            a = jnp.dot(rows, w1[e, :, cols], preferred_element_type=F32)
            b = jnp.dot(rows, w3[e, :, cols], preferred_element_type=F32)
            hid[:, cols] = (a * jax.nn.sigmoid(a) * b).astype(BF16)
            return c2

        lax.fori_loop(0, d_expert // n1, up, 0)
        copies[2].wait()

        def down(t, c2):
            cols = pl.ds(pl.multiple_of(t * n2, n2), n2)
            o = jnp.dot(hid[...], w2[e, :, cols], preferred_element_type=F32).astype(BF16)
            xo[e, :, :, :, cols] = o.reshape(side, side, CORES * cap, n2)
            return c2

        for h in range(2):
            lax.fori_loop(h * half // n2, (h + 1) * half // n2, down, 0)
            for k in near:
                for cm in range(CORES):
                    r1_copy(h, e, k, cm).start()
            r1_partner(h, e).start()
            cols = pl.ds(pl.multiple_of(h * half + core * quarter, quarter), quarter)
            mbuf[h, 0, core, e] = xo[e, my_y, :, :, cols] if h == 0 else xo[e, :, my_x, :, cols]
        return carry

    lax.fori_loop(0, local_experts, expert, 0)

    def r2_place(h, k):
        if h == 0:
            return my_y, ring(my_x, k)
        return ring(my_y, k), my_x

    def r2_copy(h, k, cd):
        y, x = r2_place(h, k)
        return remote(pbuf.at[h, k, cd], ybuf.at[h, k, core], r2_ssem.at[h, k, cd], r2_rsem.at[h, k, core], dev(y, x, cd))

    def r2_partner(h):
        return remote(pbuf.at[h, 0, 1 - core], ybuf.at[h, 0, core], r2_ssem.at[h, 0, 0], r2_rsem.at[h, 0, core], partner)

    def merge(h, k):
        y, x = r2_place(h, k)
        p = chip_at(y, x)
        q = x if h == 0 else y
        lhs = []
        for j in range(side):
            sy, sx = r1_place(h, side - j)
            base = pl.multiple_of(chip_at(sy, sx) * chip_experts, chip_experts)
            hit = slots[p, pl.ds(base, chip_experts), :][:, None, :] == wanted[None]
            g = gates[p, pl.ds(base, chip_experts), :]
            g_hi = g.astype(BF16).astype(F32)
            g_mid = (g - g_hi).astype(BF16).astype(F32)
            g_lo = g - g_hi - g_mid
            lhs.append(jnp.concatenate([
                jnp.where(hit, v[:, None, :], 0.0).reshape(chip_experts * CORES * cap, LANES).astype(BF16) for v in (g_hi, g_mid, g_lo)], axis=1))
        rows = mbuf[h, :, :, :, q].reshape(side * CORES * local_experts * CORES * cap, quarter)
        out = lax.dot_general(jnp.concatenate(lhs, axis=0), rows, (((0,), (0,)), ((), ())), preferred_element_type=F32)
        total = out[:LANES] + (out[LANES:2 * LANES] + out[2 * LANES:])
        pbuf[h, k] = total.reshape(CORES, num_tokens, quarter)

    def r1_arrived(h, k, c, e):
        pltpu.make_async_copy(mbuf.at[h, k, c, e], mbuf.at[h, k, c, e], r1_rsem.at[h, k, c, e]).wait()

    for h in range(2):
        def arrived(e, carry):
            for k in range(1, side):
                for c in range(CORES):
                    r1_arrived(h, k, c, e)
            r1_arrived(h, 0, 1 - core, e)
            return carry

        lax.fori_loop(0, local_experts, arrived, 0)

        def merge_remote(k, carry):
            merge(h, k)
            for cd in range(CORES):
                r2_copy(h, k, cd).start()
            return carry

        lax.fori_loop(1, side, merge_remote, 0)
        merge(h, 0)
        r2_partner(h).start()
        ybuf[h, 0, core] = pbuf[h, 0, core]

    for h in range(2):
        for k in near:
            for c in range(CORES):
                pltpu.make_async_copy(ybuf.at[h, k, c], ybuf.at[h, k, c], r2_rsem.at[h, k, c]).wait()
        pltpu.make_async_copy(ybuf.at[h, 0, 1 - core], ybuf.at[h, 0, 1 - core], r2_rsem.at[h, 0, 1 - core]).wait()
        for c in range(CORES):
            total = ybuf[h, 0, c]
            for k in range(1, side):
                total = total + ybuf[h, k, c]
            y_ref[:, pl.ds(h * half + c * quarter, quarter)] = total.astype(BF16)

    lax.fori_loop(1, num_devices, sent_meta, 0)

    def sent_blocks(a, carry):
        for h in range(2):
            for k in (1, side - 1):
                second_copy(h, a, k).wait_send()
            for b in range(side):
                core_copy(h, a, b).wait_send()
        return carry

    lax.fori_loop(0, side, sent_blocks, 0)
    for h in range(2):
        for k in range(1, side):
            first_copy(h, k).wait_send()
        for a in range(side):
            relay_copy(h, a, 1 if a < far else side - 1).wait_send()

    def sent_r1(e, carry):
        for h in range(2):
            for k in near:
                for cm in range(CORES):
                    r1_copy(h, e, k, cm).wait_send()
            r1_partner(h, e).wait_send()
        return carry

    lax.fori_loop(0, local_experts, sent_r1, 0)
    for h in range(2):
        for k in near:
            for cd in range(CORES):
                r2_copy(h, k, cd).wait_send()
        r2_partner(h).wait_send()


def solution(mesh):
    num_devices = mesh.shape['ep']
    side = math.isqrt(num_devices // CORES)
    row_spec = P(('dp', 'ep'), None)
    expert_spec = P('ep', None, None)

    def device_step(tokens, routes, w_router, w_one, w_three, w_two):
        num_tokens, d_model = tokens.shape
        top_k = routes.shape[1]
        num_experts = w_router.shape[1]
        local_experts, _, d_expert = w_one.shape
        cap = slot_capacity(num_tokens, top_k, num_experts)
        half = d_model // 2
        quarter = half // CORES
        chips = side * side
        any_spec = pl.BlockSpec(memory_space=pl.ANY)
        vmem_spec = pl.BlockSpec(memory_space=pltpu.VMEM)
        dma = pltpu.SemaphoreType.DMA
        return pl.pallas_call(
            functools.partial(moe_kernel, side),
            out_shape=jax.ShapeDtypeStruct((num_tokens, d_model), BF16),
            in_specs=[any_spec, vmem_spec, any_spec, any_spec, any_spec, any_spec],
            out_specs=vmem_spec,
            scratch_shapes=[
                pltpu.VMEM((2, num_devices, num_tokens, half), BF16),
                pltpu.VMEM((d_model, num_experts), BF16),
                pltpu.VMEM((local_experts, d_model, d_expert), BF16),
                pltpu.VMEM((local_experts, d_model, d_expert), BF16),
                pltpu.VMEM((local_experts, d_expert, d_model), BF16),
                pltpu.VMEM((local_experts, side, side, CORES * cap, d_model), BF16),
                pltpu.VMEM((chips * CORES * cap, d_expert), BF16),
                pltpu.VMEM((num_devices, 2 * top_k, LANES), F32),
                pltpu.VMEM((chips, num_experts, LANES), F32),
                pltpu.VMEM((chips, num_experts, LANES), F32),
                pltpu.VMEM((2, side, CORES, local_experts, side, CORES * cap, quarter), BF16),
                pltpu.VMEM((2, side, CORES, num_tokens, quarter), F32),
                pltpu.VMEM((2, side, CORES, num_tokens, quarter), F32),
                dma((2,)), dma((1,)), dma((3, local_experts)),
                dma((num_devices,)), dma((num_devices,)),
                dma((2, side)), dma((2, side, side)), dma((2, side)), dma((2, side, side)), dma((2, num_devices)),
                dma((2, side, CORES, local_experts)), dma((2, side, CORES, local_experts)),
                dma((2, side, CORES)), dma((2, side, CORES)),
            ],
            compiler_params=pltpu.CompilerParams(collective_id=0, has_side_effects=True, vmem_limit_bytes=67043328),
        )(tokens, routes.T, w_router, w_one, w_three, w_two)

    return jax.shard_map(device_step, mesh=mesh, in_specs=(row_spec, row_spec, P(None, None), expert_spec, expert_spec, expert_spec), out_specs=row_spec, check_vma=False)
```

time: 188 us -> 96.7 us (0.51)
  the two profiles are of different devices: /device:TPU:103 before, /device:TPU:97 now
where the time goes in v1:
time: 96.7 us; the launch traced here: 96.6 us
  Pallas kernels  94.9 us (98%)
  local copies, waits for them, and re-layouts  1.67 us (2%)
    pallas_call x1, Pallas kernels, device_step(): pl.pallas_call(functools.partial(moe_kernel, side), out_shape=jax.ShapeDt...  94.9 us

profile of v1, /device:TPU:97, one launch (start us, length us, event | category | flops | bytes accessed | tf_op | source)
XLA Modules:
  0.0 96.6 jit_solution(7934595611414053105)
XLA Ops:
  0.0 94.9 %shard_map.64 = bf16[64,2048]{1,0:T(8,128)(2,1)} custom-call(bf16[64,2048]{1,0:T(8,128)(2,1)} %x_hbm.1, s32[8,64]{1,0:T(8,128)} %bitcast.1, bf16[2048,128]{1,0:T(8,128)(2,1)} %wr_hbm.1, bf16[4,2048,768]{2,1,0:T(8,128)(2,1)} %w1_hbm.1, bf16[4,2048,768]{2,1,0:T(8,128)(2,1)} %w3_hbm.1, bf16[4,768,2048]{2,1,0:T(8,128)(2,1)} %w2_hbm.1), custom_call_target="tpu_custom_call" | custom-call | tf_op jit(solution)/shard_map/pallas_call | solution.py:411
  94.9 1.7 %copy.8 = bf16[64,2048]{1,0:T(8,128)(2,1)} copy(bf16[64,2048]{1,0:T(8,128)(2,1)} %shard_map.64) | data formatting | bytes 524288

commit v2 on v1

v2 whole, which is shorter than its diff:
```python
import functools
import math

import jax
import jax.numpy as jnp
from jax import lax
from jax.experimental import pallas as pl
from jax.experimental.pallas import tpu as pltpu
from jax.sharding import PartitionSpec as P

MESH = pl.DeviceIdType.MESH
F32 = jnp.float32
BF16 = jnp.bfloat16
CORES = 2
LANES = 128


def slot_capacity(num_tokens, top_k, num_experts):
    return 8 * ((3 * num_tokens * top_k + 16 * num_experts - 1) // (16 * num_experts))


def moe_kernel(
    side,
    x_hbm, routes_ref, wr_hbm, w1_hbm, w3_hbm, w2_hbm, y_ref,
    xg, wr, w13, w2, xo, hid, meta, slots, gates, mbuf, pbuf, ybuf,
    x_sem, wr_sem, w_sem, meta_ssem, meta_rsem, ag_ssem, ag_rsem, core_rsem,
    r1_ssem, r1_rsem, r2_ssem, r2_rsem,
):
    num_devices = CORES * side * side
    chips = side * side
    num_tokens, d_model = x_hbm.shape
    half = d_model // 2
    quarter = half // CORES
    local_experts, _, _, d_expert = w13.shape
    chip_experts = CORES * local_experts
    num_experts = num_devices * local_experts
    top_k = routes_ref.shape[0]
    cap = xo.shape[3] // CORES

    me = lax.axis_index('ep')
    core = lax.rem(me, CORES)
    my_x = lax.rem(lax.div(me, CORES), side)
    my_y = lax.div(me, CORES * side)

    def ring(v, k):
        return lax.rem(v + k, side)

    def chip_at(y, x):
        return y * side + x

    def dev(y, x, c):
        return chip_at(y, x) * CORES + c

    partner = dev(my_y, my_x, 1 - core)

    def remote(src, dst, ssem, rsem, target):
        return pltpu.make_async_remote_copy(src_ref=src, dst_ref=dst, send_sem=ssem, recv_sem=rsem, device_id={'ep': target}, device_id_type=MESH)

    barrier = pltpu.get_barrier_semaphore()

    def greet(i, carry):
        pl.semaphore_signal(barrier, inc=1, device_id={'ep': lax.rem(me + i, num_devices)}, device_id_type=MESH)
        return carry

    lax.fori_loop(1, num_devices, greet, 0)

    x_copies = [pltpu.make_async_copy(x_hbm.at[:, pl.ds(h * half, half)], xg.at[h, me], x_sem) for h in range(2)]
    for cp in x_copies:
        cp.start()
    wr_copy = pltpu.make_async_copy(wr_hbm, wr, wr_sem)
    wr_copy.start()

    def weight_copies(e):
        return [
            pltpu.make_async_copy(w1_hbm.at[e], w13.at[e, 0], w_sem.at[0, e]),
            pltpu.make_async_copy(w3_hbm.at[e], w13.at[e, 1], w_sem.at[0, e]),
            pltpu.make_async_copy(w2_hbm.at[e], w2.at[e], w_sem.at[1, e]),
        ]

    def start_weights(e, carry):
        for cp in weight_copies(e):
            cp.start()
        return carry

    lax.fori_loop(0, local_experts, start_weights, 0)


    pltpu.make_async_copy(xg.at[:, me], xg.at[:, me], x_sem).wait()

    wr_copy.wait()
    x_local = [xg[h, me] for h in range(2)]
    logits = sum(
        lax.dot_general(wr[pl.ds(h * half, half), :], x_local[h], (((0,), (1,)), ((), ())), preferred_element_type=F32)
        for h in range(2)
    )
    routes = routes_ref[...]
    expert_iota = lax.broadcasted_iota(jnp.int32, (num_experts, num_tokens), 0)
    picked = jnp.concatenate(
        [jnp.sum(jnp.where(expert_iota == routes[j:j + 1, :], logits, 0.0), axis=0, keepdims=True) for j in range(top_k)], axis=0)
    ex = jnp.exp(picked - jnp.max(picked, axis=0, keepdims=True))
    gate = ex / jnp.sum(ex, axis=0, keepdims=True)
    meta[me] = jnp.concatenate([routes.astype(F32) + 1.0, gate], axis=1)

    pl.semaphore_wait(barrier, num_devices - 1)

    def place(h, a, b):
        if h == 0:
            return ring(my_y, b), ring(my_x, a)
        return ring(my_y, a), ring(my_x, b)

    def block_src(h, a, b, c):
        y, x = place(h, a, b)
        return dev(y, x, c)

    def move_block(h, src, rsem, target):
        return remote(xg.at[h, src], xg.at[h, src], ag_ssem.at[h], rsem, target)

    def first_copy(h, k):
        return move_block(h, me, ag_rsem.at[side - k, 0], block_src(h, k, 0, core))

    def second_copy(h, a, k):
        return move_block(h, block_src(h, a, 0, core), ag_rsem.at[a, side - k], block_src(h, 0, k, core))

    def relay_copy(h, a, k):
        return move_block(h, block_src(h, a, k, core), ag_rsem.at[a, side // 2], block_src(h, 0, side - k, core))

    def core_copy(h, a, b):
        return move_block(h, block_src(h, a, b, core), core_rsem.at[a, b], partner)

    def wait_blocks(sem):
        pltpu.make_async_copy(xg.at[:, me], xg.at[:, me], sem).wait()

    def meta_copy(i):
        return remote(meta.at[me], meta.at[me], meta_ssem, meta_rsem, lax.rem(me + i, num_devices))

    def send_meta(i, carry):
        meta_copy(i).start()
        return carry

    def wait_meta(sem):
        others = meta.at[pl.ds(0, num_devices - 1)]
        pltpu.make_async_copy(others, others, sem).wait()

    lax.fori_loop(1, num_devices, send_meta, 0)
    for h in range(2):
        for k in (1, side - 1) + tuple(range(2, side - 1)):
            first_copy(h, k).start()
        for k in (1, side - 1):
            second_copy(h, 0, k).start()
        core_copy(h, 0, 0).start()

    row_i = lax.broadcasted_iota(jnp.int32, (LANES, LANES), 0)
    col_i = lax.broadcasted_iota(jnp.int32, (LANES, LANES), 1)
    before = jnp.where((row_i < col_i) & (row_i // num_tokens == col_i // num_tokens), 1.0, 0.0).astype(BF16)
    ids = lax.broadcasted_iota(jnp.int32, (num_experts, LANES), 0).astype(F32) + 1.0

    def plan_chip(p, carry):
        tiles = [meta[CORES * p + c] for c in range(CORES)]
        turned = [pltpu.roll(v, num_tokens, 1) for v in tiles]
        low = lax.broadcasted_iota(jnp.int32, tiles[0].shape, 1) < num_tokens
        picks = jnp.where(low, tiles[0], turned[1])
        shares = jnp.where(low, turned[0], tiles[1])
        mask = jnp.zeros((num_experts, LANES), F32)
        weight = jnp.zeros((num_experts, LANES), F32)
        for j in range(top_k):
            hit = ids == picks[j:j + 1, :]
            mask = jnp.where(hit, 1.0, mask)
            weight = jnp.where(hit, shares[j:j + 1, :], weight)
        rank = jnp.dot(mask.astype(BF16), before, preferred_element_type=F32)
        slots[p] = jnp.where(mask > 0.0, rank, -1.0)
        gates[p] = weight
        return carry


    pair_row = lax.broadcasted_iota(jnp.int32, (CORES * cap, LANES), 0)
    pair_lane = lax.broadcasted_iota(jnp.int32, (CORES * cap, LANES), 1)
    wanted = jnp.where(pair_row // cap == pair_lane // num_tokens, pair_row % cap, -2).astype(F32)

    def gather_chip(h, y, x):
        p = chip_at(y, x)
        mine = slots[p, pl.ds(me * local_experts, local_experts), :]
        pick = jnp.where(mine[:, None, :] == wanted[None], 1.0, 0.0).reshape(local_experts * CORES * cap, LANES).astype(BF16)
        rows = xg[h, pl.ds(p * CORES, CORES)].reshape(CORES * num_tokens, half)
        out = jnp.dot(pick, rows, preferred_element_type=F32).astype(BF16)
        xo[:, y, x, :, pl.ds(h * half, half)] = out.reshape(local_experts, CORES * cap, half)

    def finish(a, b):
        wait_blocks(core_rsem.at[a, b])
        for h in range(2):
            gather_chip(h, *place(h, a, b))

    def land(a, b):
        wait_blocks(ag_rsem.at[a, b])
        for h in range(2):
            core_copy(h, a, b).start()

    far = side // 2
    near = (1, side - 1) + tuple(range(2, side - 1))

    def same_line(a):
        land(a, 0)
        for h in range(2):
            for k in (1, side - 1):
                second_copy(h, a, k).start()

    def next_lines(a, carry):
        land(a, 1)
        for h in range(2):
            relay_copy(h, a, 1).start()
        land(a + far, side - 1)
        for h in range(2):
            relay_copy(h, a + far, side - 1).start()
        land(a + far, 1)
        land(a, side - 1)
        finish(a, 0)
        finish(a + far, 0)
        return carry

    def far_line(a, carry):
        land(a, far)
        finish(a, 1)
        finish(a, side - 1)
        return carry

    def far_lines(a, carry):
        far_line(a, carry)
        finish(a - 1, far)
        return carry

    for a in near:
        same_line(a)
    wait_meta(meta_rsem)
    lax.fori_loop(0, chips, plan_chip, 0)
    lax.fori_loop(0, far, next_lines, 0)
    far_line(0, 0)
    lax.fori_loop(1, side, far_lines, 0)
    finish(side - 1, far)

    def r1_place(h, k):
        if h == 0:
            return ring(my_y, k), my_x
        return my_y, ring(my_x, k)

    def r1_src(h, e, k, cm):
        y, x = r1_place(h, k)
        cols = pl.ds(h * half + cm * quarter, quarter)
        if h == 0:
            return xo.at[e, y, :, :, cols]
        return xo.at[e, :, x, :, cols]

    def r1_copy(h, e, k, cm):
        y, x = r1_place(h, k)
        return remote(r1_src(h, e, k, cm), mbuf.at[h, k, core, e], r1_ssem.at[0], r1_rsem.at[h, k], dev(y, x, cm))

    def r1_partner(h, e):
        y, x = my_y, my_x
        cols = pl.ds(pl.multiple_of(h * half + (1 - core) * quarter, quarter), quarter)
        src = xo.at[e, y, :, :, cols] if h == 0 else xo.at[e, :, x, :, cols]
        return remote(src, mbuf.at[h, 0, core, e], r1_ssem.at[1], r1_rsem.at[h, 0], partner)

    n1 = 256
    n2 = 512

    def expert(e, carry):
        pltpu.make_async_copy(w13.at[e], w13.at[e], w_sem.at[0, e]).wait()

        def up(t, c2):
            rows = xo[e].reshape(chips * CORES * cap, d_model)
            cols = pl.ds(pl.multiple_of(t * n1, n1), n1)
            a = jnp.dot(rows, w13[e, 0, :, cols], preferred_element_type=F32)
            b = jnp.dot(rows, w13[e, 1, :, cols], preferred_element_type=F32)
            hid[:, cols] = (a * jax.nn.sigmoid(a) * b).astype(BF16)
            return c2

        lax.fori_loop(0, d_expert // n1, up, 0)
        weight_copies(e)[2].wait()

        def down(t, c2):
            cols = pl.ds(pl.multiple_of(t * n2, n2), n2)
            o = jnp.dot(hid[...], w2[e, :, cols], preferred_element_type=F32).astype(BF16)
            xo[e, :, :, :, cols] = o.reshape(side, side, CORES * cap, n2)
            return c2

        for h in range(2):
            lax.fori_loop(h * half // n2, (h + 1) * half // n2, down, 0)
            for k in near:
                for cm in range(CORES):
                    r1_copy(h, e, k, cm).start()
            r1_partner(h, e).start()
            cols = pl.ds(pl.multiple_of(h * half + core * quarter, quarter), quarter)
            mbuf[h, 0, core, e] = xo[e, my_y, :, :, cols] if h == 0 else xo[e, :, my_x, :, cols]
        return carry

    lax.fori_loop(0, local_experts, expert, 0)

    def r2_place(h, k):
        if h == 0:
            return my_y, ring(my_x, k)
        return ring(my_y, k), my_x

    def r2_copy(h, k, cd):
        y, x = r2_place(h, k)
        return remote(pbuf.at[h, k, cd], ybuf.at[h, k, core], r2_ssem.at[0], r2_rsem.at[h, 0], dev(y, x, cd))

    def r2_partner(h):
        return remote(pbuf.at[h, 0, 1 - core], ybuf.at[h, 0, core], r2_ssem.at[1], r2_rsem.at[h, 1], partner)

    def merge(h, k):
        y, x = r2_place(h, k)
        p = chip_at(y, x)
        q = x if h == 0 else y
        lhs = []
        for j in range(side):
            sy, sx = r1_place(h, side - j)
            base = pl.multiple_of(chip_at(sy, sx) * chip_experts, chip_experts)
            hit = slots[p, pl.ds(base, chip_experts), :][:, None, :] == wanted[None]
            g = gates[p, pl.ds(base, chip_experts), :]
            g_hi = g.astype(BF16).astype(F32)
            g_mid = (g - g_hi).astype(BF16).astype(F32)
            g_lo = g - g_hi - g_mid
            lhs.append(jnp.concatenate([
                jnp.where(hit, v[:, None, :], 0.0).reshape(chip_experts * CORES * cap, LANES).astype(BF16) for v in (g_hi, g_mid, g_lo)], axis=1))
        rows = mbuf[h, :, :, :, q].reshape(side * CORES * local_experts * CORES * cap, quarter)
        out = lax.dot_general(jnp.concatenate(lhs, axis=0), rows, (((0,), (0,)), ((), ())), preferred_element_type=F32)
        total = out[:LANES] + (out[LANES:2 * LANES] + out[2 * LANES:])
        pbuf[h, k] = total.reshape(CORES, num_tokens, quarter)

    def wait_bytes(ref, sem):
        pltpu.make_async_copy(ref, ref, sem).wait()

    for h in range(2):
        for k in range(1, side):
            wait_bytes(mbuf.at[h, k], r1_rsem.at[h, k])
        wait_bytes(mbuf.at[h, 0, 1 - core], r1_rsem.at[h, 0])

    def merge_remote(i, carry):
        k = lax.rem(i + 1, side - 1) + 1
        for h in range(2):
            merge(h, k)
            for cd in range(CORES):
                r2_copy(h, k, cd).start()
        return carry

    lax.fori_loop(0, side - 1, merge_remote, 0)
    for h in range(2):
        merge(h, 0)
        r2_partner(h).start()
        ybuf[h, 0, core] = pbuf[h, 0, core]

    for h in range(2):
        wait_bytes(ybuf.at[h, pl.ds(1, side - 1)], r2_rsem.at[h, 0])
        wait_bytes(ybuf.at[h, 0, 1 - core], r2_rsem.at[h, 1])
        for c in range(CORES):
            total = ybuf[h, 0, c]
            for k in range(1, side):
                total = total + ybuf[h, k, c]
            y_ref[:, pl.ds(h * half + c * quarter, quarter)] = total.astype(BF16)

    wait_meta(meta_ssem)
    for h in range(2):
        wait_bytes(xg.at[h, pl.ds(0, side - 1 + 2 * side + side + chips)], ag_ssem.at[h])
    wait_bytes(mbuf.at[:, pl.ds(1, side - 1)], r1_ssem.at[0])
    wait_bytes(mbuf.at[:, 0, 0], r1_ssem.at[1])
    wait_bytes(pbuf.at[:, pl.ds(1, side - 1)], r2_ssem.at[0])
    wait_bytes(pbuf.at[:, 0, 0], r2_ssem.at[1])


def solution(mesh):
    num_devices = mesh.shape['ep']
    side = math.isqrt(num_devices // CORES)
    row_spec = P(('dp', 'ep'), None)
    expert_spec = P('ep', None, None)

    def device_step(tokens, routes, w_router, w_one, w_three, w_two):
        num_tokens, d_model = tokens.shape
        top_k = routes.shape[1]
        num_experts = w_router.shape[1]
        local_experts, _, d_expert = w_one.shape
        cap = slot_capacity(num_tokens, top_k, num_experts)
        half = d_model // 2
        quarter = half // CORES
        chips = side * side
        any_spec = pl.BlockSpec(memory_space=pl.ANY)
        vmem_spec = pl.BlockSpec(memory_space=pltpu.VMEM)
        dma = pltpu.SemaphoreType.DMA
        return pl.pallas_call(
            functools.partial(moe_kernel, side),
            out_shape=jax.ShapeDtypeStruct((num_tokens, d_model), BF16),
            in_specs=[any_spec, vmem_spec, any_spec, any_spec, any_spec, any_spec],
            out_specs=vmem_spec,
            scratch_shapes=[
                pltpu.VMEM((2, num_devices, num_tokens, half), BF16),
                pltpu.VMEM((d_model, num_experts), BF16),
                pltpu.VMEM((local_experts, 2, d_model, d_expert), BF16),
                pltpu.VMEM((local_experts, d_expert, d_model), BF16),
                pltpu.VMEM((local_experts, side, side, CORES * cap, d_model), BF16),
                pltpu.VMEM((chips * CORES * cap, d_expert), BF16),
                pltpu.VMEM((num_devices, top_k, LANES), F32),
                pltpu.VMEM((chips, num_experts, LANES), F32),
                pltpu.VMEM((chips, num_experts, LANES), F32),
                pltpu.VMEM((2, side, CORES, local_experts, side, CORES * cap, quarter), BF16),
                pltpu.VMEM((2, side, CORES, num_tokens, quarter), F32),
                pltpu.VMEM((2, side, CORES, num_tokens, quarter), F32),
                dma, dma, dma((2, local_experts)), dma, dma, dma((2,)), dma((side, side)), dma((side, side)),
                dma((2,)), dma((2, side)), dma((2,)), dma((2, 2)),
            ],
            compiler_params=pltpu.CompilerParams(collective_id=0, has_side_effects=True, vmem_limit_bytes=67043328),
        )(tokens, routes.T, w_router, w_one, w_three, w_two)

    return jax.shard_map(device_step, mesh=mesh, in_specs=(row_spec, row_spec, P(None, None), expert_spec, expert_spec, expert_spec), out_specs=row_spec, check_vma=False)
```

time: 96.7 us -> 85.2 us (0.88)
  Pallas kernels: 94.9 us -> 83.3 us
    pallas_call x1, Pallas kernels: 94.9 us -> 83.3 us  [device_step(): pl.pallas_call(functools.partial(moe_kernel, side), out_shape=jax.ShapeDt...]
where the time goes in v2:
time: 85.2 us; the launch traced here: 85 us
  Pallas kernels  83.3 us (98%)
  local copies, waits for them, and re-layouts  1.67 us (2%)
    pallas_call x1, Pallas kernels, device_step(): pl.pallas_call(functools.partial(moe_kernel, side), out_shape=jax.ShapeDt...  83.3 us

profile of v2, /device:TPU:97, one launch (start us, length us, event | category | flops | bytes accessed | tf_op | source)
XLA Modules:
  0.0 85.0 jit_solution(44467673986588803)
XLA Ops:
  0.0 83.3 %shard_map.64 = bf16[64,2048]{1,0:T(8,128)(2,1)} custom-call(bf16[64,2048]{1,0:T(8,128)(2,1)} %x_hbm.1, s32[8,64]{1,0:T(8,128)} %bitcast.1, bf16[2048,128]{1,0:T(8,128)(2,1)} %wr_hbm.1, bf16[4,2048,768]{2,1,0:T(8,128)(2,1)} %w1_hbm.1, bf16[4,2048,768]{2,1,0:T(8,128)(2,1)} %w3_hbm.1, bf16[4,768,2048]{2,1,0:T(8,128)(2,1)} %w2_hbm.1), custom_call_target="tpu_custom_call" | custom-call | tf_op jit(solution)/shard_map/pallas_call | solution.py:386
  83.4 1.7 %copy.8 = bf16[64,2048]{1,0:T(8,128)(2,1)} copy(bf16[64,2048]{1,0:T(8,128)(2,1)} %shard_map.64) | data formatting | bytes 524288

commit v3 on v2

v3 whole, which is shorter than its diff:
```python
import functools
import math

import jax
import jax.numpy as jnp
from jax import lax
from jax.experimental import pallas as pl
from jax.experimental.pallas import tpu as pltpu
from jax.sharding import PartitionSpec as P

MESH = pl.DeviceIdType.MESH
F32 = jnp.float32
BF16 = jnp.bfloat16
CORES = 2
LANES = 128


def slot_capacity(num_tokens, top_k, num_experts):
    return 8 * ((3 * num_tokens * top_k + 16 * num_experts - 1) // (16 * num_experts))


def moe_kernel(
    side,
    x_hbm, routes_hbm, wr_hbm, w1_hbm, w3_hbm, w2_hbm, y_ref,
    xg, routes_ref, wr, w13, w2, xo, hid, meta, slots, gates, mbuf, pbuf, ybuf,
    x_sem, wr_sem, routes_sem, w_sem, meta_ssem, meta_rsem, ag_ssem, ag_rsem, core_rsem,
    r1_ssem, r1_rsem, r2_ssem, r2_rsem,
):
    num_devices = CORES * side * side
    chips = side * side
    num_tokens, d_model = x_hbm.shape
    half = d_model // 2
    quarter = half // CORES
    piece = quarter // 2
    local_experts, _, _, d_expert = w13.shape
    chip_experts = CORES * local_experts
    num_experts = num_devices * local_experts
    top_k = routes_ref.shape[0]
    cap = xo.shape[3] // CORES

    me = lax.axis_index('ep')
    core = lax.rem(me, CORES)
    my_x = lax.rem(lax.div(me, CORES), side)
    my_y = lax.div(me, CORES * side)

    def ring(v, k):
        return lax.rem(v + k, side)

    far = side // 2

    def spot(k):
        return k + (k // far) * (side + 1 - 2 * k)

    def chip_at(y, x):
        return y * side + x

    def dev(y, x, c):
        return chip_at(y, x) * CORES + c

    partner = dev(my_y, my_x, 1 - core)

    def remote(src, dst, ssem, rsem, target):
        return pltpu.make_async_remote_copy(src_ref=src, dst_ref=dst, send_sem=ssem, recv_sem=rsem, device_id={'ep': target}, device_id_type=MESH)

    barrier = pltpu.get_barrier_semaphore()

    def greet(i, carry):
        pl.semaphore_signal(barrier, inc=1, device_id={'ep': lax.rem(me + i, num_devices)}, device_id_type=MESH)
        return carry

    lax.fori_loop(1, num_devices, greet, 0)

    x_copies = [pltpu.make_async_copy(x_hbm.at[:, pl.ds(h * half, half)], xg.at[h, me], x_sem) for h in range(2)]
    for cp in x_copies:
        cp.start()
    wr_copy = pltpu.make_async_copy(wr_hbm, wr, wr_sem)
    wr_copy.start()
    routes_copy = pltpu.make_async_copy(routes_hbm, routes_ref, routes_sem)
    routes_copy.start()

    def weight_copies(e):
        return [
            pltpu.make_async_copy(w1_hbm.at[e], w13.at[e, 0], w_sem.at[0, e]),
            pltpu.make_async_copy(w3_hbm.at[e], w13.at[e, 1], w_sem.at[0, e]),
            pltpu.make_async_copy(w2_hbm.at[e], w2.at[e], w_sem.at[1, e]),
        ]

    def start_weights(e, carry):
        for cp in weight_copies(e):
            cp.start()
        return carry

    lax.fori_loop(0, local_experts, start_weights, 0)


    pltpu.make_async_copy(xg.at[:, me], xg.at[:, me], x_sem).wait()

    wr_copy.wait()
    routes_copy.wait()
    x_local = [xg[h, me] for h in range(2)]
    logits = sum(
        lax.dot_general(wr[pl.ds(h * half, half), :], x_local[h], (((0,), (1,)), ((), ())), preferred_element_type=F32)
        for h in range(2)
    )
    routes = routes_ref[...]
    expert_iota = lax.broadcasted_iota(jnp.int32, (num_experts, num_tokens), 0)
    picked = jnp.concatenate(
        [jnp.sum(jnp.where(expert_iota == routes[j:j + 1, :], logits, 0.0), axis=0, keepdims=True) for j in range(top_k)], axis=0)
    ex = jnp.exp(picked - jnp.max(picked, axis=0, keepdims=True))
    gate = ex / jnp.sum(ex, axis=0, keepdims=True)
    meta[me] = jnp.concatenate([routes.astype(F32) + 1.0, gate], axis=1)

    pl.semaphore_wait(barrier, num_devices - 1)

    def place(h, a, b):
        if h == 0:
            return ring(my_y, b), ring(my_x, a)
        return ring(my_y, a), ring(my_x, b)

    def block_src(h, a, b, c):
        y, x = place(h, a, b)
        return dev(y, x, c)

    def move_block(h, src, rsem, target):
        return remote(xg.at[h, src], xg.at[h, src], ag_ssem.at[h], rsem, target)

    def first_copy(h, k):
        return move_block(h, me, ag_rsem.at[side - k, 0], block_src(h, k, 0, core))

    def first_relay(h):
        k = 1 + core * (side - 2)
        return move_block(h, block_src(h, k, 0, core), ag_rsem.at[side // 2, 0], block_src(h, side - k, 0, core))

    def second_copy(h, a, k):
        return move_block(h, block_src(h, a, 0, core), ag_rsem.at[a, side - k], block_src(h, 0, k, core))

    def relay_copy(h, a, k):
        return move_block(h, block_src(h, a, k, core), ag_rsem.at[a, side // 2], block_src(h, 0, side - k, core))

    def core_copy(h, a, b):
        return move_block(h, block_src(h, a, b, core), core_rsem.at[a, b], partner)

    def wait_blocks(sem):
        pltpu.make_async_copy(xg.at[:, me], xg.at[:, me], sem).wait()

    def meta_copy(i):
        return remote(meta.at[me], meta.at[me], meta_ssem, meta_rsem, lax.rem(me + i, num_devices))

    def send_meta(i, carry):
        meta_copy(i).start()
        return carry

    def wait_meta(sem):
        others = meta.at[pl.ds(0, num_devices - 1)]
        pltpu.make_async_copy(others, others, sem).wait()

    for h in range(2):
        for k in (1, side - 1):
            first_copy(h, k).start()
    lax.fori_loop(1, num_devices, send_meta, 0)
    for h in range(2):
        for k in (1, side - 1):
            second_copy(h, 0, k).start()
        core_copy(h, 0, 0).start()

    row_i = lax.broadcasted_iota(jnp.int32, (LANES, LANES), 0)
    col_i = lax.broadcasted_iota(jnp.int32, (LANES, LANES), 1)
    before = jnp.where((row_i < col_i) & (row_i // num_tokens == col_i // num_tokens), 1.0, 0.0).astype(BF16)
    ids = lax.broadcasted_iota(jnp.int32, (num_experts, LANES), 0).astype(F32) + 1.0

    def plan_chip(p, carry):
        tiles = [meta[CORES * p + c] for c in range(CORES)]
        turned = [pltpu.roll(v, num_tokens, 1) for v in tiles]
        low = lax.broadcasted_iota(jnp.int32, tiles[0].shape, 1) < num_tokens
        picks = jnp.where(low, tiles[0], turned[1])
        shares = jnp.where(low, turned[0], tiles[1])
        mask = jnp.zeros((num_experts, LANES), F32)
        weight = jnp.zeros((num_experts, LANES), F32)
        for j in range(top_k):
            hit = ids == picks[j:j + 1, :]
            mask = jnp.where(hit, 1.0, mask)
            weight = jnp.where(hit, shares[j:j + 1, :], weight)
        rank = jnp.dot(mask.astype(BF16), before, preferred_element_type=F32)
        slots[p] = jnp.where(mask > 0.0, rank, -1.0)
        gates[p] = weight
        return carry


    pair_row = lax.broadcasted_iota(jnp.int32, (CORES * cap, LANES), 0)
    pair_lane = lax.broadcasted_iota(jnp.int32, (CORES * cap, LANES), 1)
    wanted = jnp.where(pair_row // cap == pair_lane // num_tokens, pair_row % cap, -2).astype(F32)

    def gather_chip(h, a, b):
        p = chip_at(*place(h, a, b))
        py, px = (spot(b), spot(a)) if h == 0 else (spot(a), spot(b))
        mine = slots[p, pl.ds(me * local_experts, local_experts), :]
        pick = jnp.where(mine[:, None, :] == wanted[None], 1.0, 0.0).reshape(local_experts * CORES * cap, LANES).astype(BF16)
        rows = xg[h, pl.ds(p * CORES, CORES)].reshape(CORES * num_tokens, half)
        out = jnp.dot(pick, rows, preferred_element_type=F32).astype(BF16)
        xo[:, py, px, :, pl.ds(h * half, half)] = out.reshape(local_experts, CORES * cap, half)

    def finish(a, b):
        wait_blocks(core_rsem.at[a, b])
        for h in range(2):
            gather_chip(h, a, b)

    def land(a, b):
        wait_blocks(ag_rsem.at[a, b])
        for h in range(2):
            core_copy(h, a, b).start()

    near = (1, side - 1) + tuple(range(2, side - 1))

    def same_line(a):
        for h in range(2):
            for k in (1, side - 1):
                second_copy(h, a, k).start()

    def next_lines(a, carry):
        land(a, 1)
        for h in range(2):
            relay_copy(h, a, 1).start()
        land(a + far, side - 1)
        for h in range(2):
            relay_copy(h, a + far, side - 1).start()
        land(a + far, 1)
        land(a, side - 1)
        finish(a, 0)
        finish(a + far, 0)
        return carry

    def near_lines(p, carry):
        finish(spot(p), 1)
        finish(spot(p), side - 1)
        return carry

    def far_lines(p, carry):
        finish(spot(p), far)
        return carry

    for a in near[:2]:
        land(a, 0)
    for h in range(2):
        first_relay(h).start()
    for a in near[:2]:
        same_line(a)
    wait_meta(meta_rsem)
    lax.fori_loop(0, chips, plan_chip, 0)
    land(far, 0)
    same_line(far)
    lax.fori_loop(0, far, next_lines, 0)
    lax.fori_loop(0, side - 1, near_lines, 0)

    def r1_place(h, k):
        if h == 0:
            return ring(my_y, k), my_x
        return my_y, ring(my_x, k)

    close, edge = pl.ds(0, side - 1), pl.ds(side - 1, 1)
    whole = pl.ds(0, side)
    n_close = (side - 1) * (side - 1) * CORES * cap
    n_rows = chips * CORES * cap
    lines = {
        'near': [(0, close)] + [(k, close) for k in (1, side - 1)],
        'far': [(0, edge)] + [(far, whole)] + [(k, edge) for k in (1, side - 1)],
        'all': [(0, whole)] + [(k, whole) for k in (far, 1, side - 1)],
    }
    spans = {'near': pl.ds(0, n_close), 'far': pl.ds(n_close, n_rows - n_close), 'all': pl.ds(0, n_rows)}

    def read_rows(part, e):
        if part == 'near':
            return xo[e, close, close].reshape(n_close, d_model)
        if part == 'far':
            n_edge = side * CORES * cap
            return jnp.concatenate([xo[e, side - 1].reshape(n_edge, d_model), xo[e, close, side - 1].reshape(n_rows - n_close - n_edge, d_model)], axis=0)
        return xo[e].reshape(n_rows, d_model)

    def write_rows(part, e, cols, o):
        n = o.shape[1]
        if part == 'near':
            xo[e, close, close, :, cols] = o.reshape(side - 1, side - 1, CORES * cap, n)
        elif part == 'far':
            n_edge = side * CORES * cap
            xo[e, side - 1, :, :, cols] = o[:n_edge].reshape(side, CORES * cap, n)
            xo[e, close, side - 1, :, cols] = o[n_edge:].reshape(side - 1, CORES * cap, n)
        else:
            xo[e, :, :, :, cols] = o.reshape(side, side, CORES * cap, n)

    def line_ref(h, e, k, span, cols):
        return xo.at[e, spot(k), span, :, cols] if h == 0 else xo.at[e, span, spot(k), :, cols]

    def cols_of(g, h, c):
        return pl.ds(pl.multiple_of(h * half + c * quarter + g * piece, piece), piece)

    def r1_copy(g, h, e, k, span, cm):
        y, x = r1_place(h, k)
        src = line_ref(h, e, k, span, cols_of(g, h, cm))
        return remote(src, mbuf.at[g, h, k, core, e, span], r1_ssem.at[0], r1_rsem.at[g, h, k], dev(y, x, cm))

    def r1_partner(g, h, e, span):
        src = line_ref(h, e, 0, span, cols_of(g, h, 1 - core))
        return remote(src, mbuf.at[g, h, 0, core, e, span], r1_ssem.at[1], r1_rsem.at[g, h, 0], partner)

    n1 = 256

    def up_rows(part, e):
        if part != 'far':
            pltpu.make_async_copy(w13.at[e], w13.at[e], w_sem.at[0, e]).wait()

        def up(t, carry):
            rows = read_rows(part, e)
            cols = pl.ds(pl.multiple_of(t * n1, n1), n1)
            a = jnp.dot(rows, w13[e, 0, :, cols], preferred_element_type=F32)
            b = jnp.dot(rows, w13[e, 1, :, cols], preferred_element_type=F32)
            hid[e % 2, spans[part], cols] = (a * jax.nn.sigmoid(a) * b).astype(BF16)
            return carry

        lax.fori_loop(0, d_expert // n1, up, 0)

    def send_rows(part, e, g, h):
        for k, span in lines[part][1:]:
            for cm in range(CORES):
                r1_copy(g, h, e, k, span, cm).start()
        span = lines[part][0][1]
        r1_partner(g, h, e, span).start()
        cols = cols_of(g, h, core)
        mbuf[g, h, 0, core, e, span] = xo[e, 0, span, :, cols] if h == 0 else xo[e, span, 0, :, cols]

    def down_group(part, e, g):
        for h in range(2):
            def down(c, carry):
                cols = cols_of(g, h, c)
                write_rows(part, e, cols, jnp.dot(hid[e % 2, spans[part], :], w2[e, :, cols], preferred_element_type=F32).astype(BF16))
                return carry

            lax.fori_loop(0, CORES, down, 0)
            send_rows(part, e, g, h)

    def wait_down(e):
        pltpu.make_async_copy(w2.at[e], w2.at[e], w_sem.at[1, e]).wait()

    def down_rows(part, e):
        if part != 'far':
            wait_down(e)

        def down(t, carry):
            cols = pl.ds(pl.multiple_of(t * quarter, quarter), quarter)
            write_rows(part, e, cols, jnp.dot(hid[e % 2, spans[part], :], w2[e, :, cols], preferred_element_type=F32).astype(BF16))
            return carry

        for h in range(2):
            lax.fori_loop(h * CORES, (h + 1) * CORES, down, 0)
            for g in range(2):
                send_rows(part, e, g, h)

    early = 2

    def near_expert(e, carry):
        up_rows('near', e)
        for i in range(far):
            land(spot(e * far + i), far)
        down_rows('near', e)
        return carry

    def far_expert(e, carry):
        up_rows('far', e)
        down_rows('far', e)
        return carry

    def all_expert(e, carry):
        up_rows('all', e)
        wait_down(e)
        down_group('all', e, 0)
        return carry

    def all_second(e, carry):
        down_group('all', e, 1)
        return carry

    lax.fori_loop(0, early, near_expert, 0)
    finish(far, 1)
    finish(far, side - 1)
    lax.fori_loop(0, side, far_lines, 0)
    lax.fori_loop(0, early, far_expert, 0)
    lax.fori_loop(early, local_experts, all_expert, 0)
    lax.fori_loop(early, local_experts, all_second, 0)

    def r2_place(h, k):
        if h == 0:
            return my_y, ring(my_x, k)
        return ring(my_y, k), my_x

    def r2_copy(g, h, k, cd):
        y, x = r2_place(h, k)
        return remote(pbuf.at[g, h, k, cd], ybuf.at[g, h, k, core], r2_ssem.at[0], r2_rsem.at[g, h, 0], dev(y, x, cd))

    def r2_partner(g, h):
        return remote(pbuf.at[g, h, 0, 1 - core], ybuf.at[g, h, 0, core], r2_ssem.at[1], r2_rsem.at[g, h, 1], partner)

    def merge(g, h, k):
        y, x = r2_place(h, k)
        p = chip_at(y, x)
        q = spot(k)
        lhs = []
        for j in range(side):
            sy, sx = r1_place(h, side - j)
            base = pl.multiple_of(chip_at(sy, sx) * chip_experts, chip_experts)
            hit = slots[p, pl.ds(base, chip_experts), :][:, None, :] == wanted[None]
            share = gates[p, pl.ds(base, chip_experts), :]
            g_hi = share.astype(BF16).astype(F32)
            g_mid = (share - g_hi).astype(BF16).astype(F32)
            g_lo = share - g_hi - g_mid
            lhs.append(jnp.concatenate([
                jnp.where(hit, v[:, None, :], 0.0).reshape(chip_experts * CORES * cap, LANES).astype(BF16) for v in (g_hi, g_mid, g_lo)], axis=1))
        rows = mbuf[g, h, :, :, :, q].reshape(side * CORES * local_experts * CORES * cap, piece)
        out = lax.dot_general(jnp.concatenate(lhs, axis=0), rows, (((0,), (0,)), ((), ())), preferred_element_type=F32)
        total = out[:LANES] + (out[LANES:2 * LANES] + out[2 * LANES:])
        pbuf[g, h, k] = total.reshape(CORES, num_tokens, piece)

    def wait_bytes(ref, sem):
        pltpu.make_async_copy(ref, ref, sem).wait()

    def merge_group(g, carry):
        for h in range(2):
            for k in range(1, side):
                wait_bytes(mbuf.at[g, h, k], r1_rsem.at[g, h, k])
            wait_bytes(mbuf.at[g, h, 0, 1 - core], r1_rsem.at[g, h, 0])

        def merge_remote(i, c2):
            k = lax.rem(i + 1, side - 1) + 1
            for h in range(2):
                merge(g, h, k)
                for cd in range(CORES):
                    r2_copy(g, h, k, cd).start()
            return c2

        lax.fori_loop(0, side - 1, merge_remote, 0)
        for h in range(2):
            merge(g, h, 0)
            r2_partner(g, h).start()
            ybuf[g, h, 0, core] = pbuf[g, h, 0, core]
        return carry

    lax.fori_loop(0, 2, merge_group, 0)

    for g in range(2):
        for h in range(2):
            wait_bytes(ybuf.at[g, h, pl.ds(1, side - 1)], r2_rsem.at[g, h, 0])
            wait_bytes(ybuf.at[g, h, 0, 1 - core], r2_rsem.at[g, h, 1])
            for c in range(CORES):
                total = ybuf[g, h, 0, c]
                for k in range(1, side):
                    total = total + ybuf[g, h, k, c]
                y_ref[:, cols_of(g, h, c)] = total.astype(BF16)

    wait_meta(meta_ssem)
    for h in range(2):
        wait_bytes(xg.at[h, pl.ds(0, side - 1 + 2 * side + side + chips)], ag_ssem.at[h])
    wait_bytes(mbuf.at[:, :, pl.ds(1, side - 1)], r1_ssem.at[0])
    wait_bytes(mbuf.at[:, :, 0, 0], r1_ssem.at[1])
    wait_bytes(pbuf.at[:, :, pl.ds(1, side - 1)], r2_ssem.at[0])
    wait_bytes(pbuf.at[:, :, 0, 0], r2_ssem.at[1])


def solution(mesh):
    num_devices = mesh.shape['ep']
    side = math.isqrt(num_devices // CORES)
    row_spec = P(('dp', 'ep'), None)
    expert_spec = P('ep', None, None)

    def device_step(tokens, routes, w_router, w_one, w_three, w_two):
        num_tokens, d_model = tokens.shape
        top_k = routes.shape[1]
        num_experts = w_router.shape[1]
        local_experts, _, d_expert = w_one.shape
        cap = slot_capacity(num_tokens, top_k, num_experts)
        half = d_model // 2
        piece = half // CORES // 2
        chips = side * side
        any_spec = pl.BlockSpec(memory_space=pl.ANY)
        vmem_spec = pl.BlockSpec(memory_space=pltpu.VMEM)
        dma = pltpu.SemaphoreType.DMA
        return pl.pallas_call(
            functools.partial(moe_kernel, side),
            out_shape=jax.ShapeDtypeStruct((num_tokens, d_model), BF16),
            in_specs=[any_spec, any_spec, any_spec, any_spec, any_spec, any_spec],
            out_specs=vmem_spec,
            scratch_shapes=[
                pltpu.VMEM((2, num_devices, num_tokens, half), BF16),
                pltpu.VMEM((top_k, num_tokens), jnp.int32),
                pltpu.VMEM((d_model, num_experts), BF16),
                pltpu.VMEM((local_experts, 2, d_model, d_expert), BF16),
                pltpu.VMEM((local_experts, d_expert, d_model), BF16),
                pltpu.VMEM((local_experts, side, side, CORES * cap, d_model), BF16),
                pltpu.VMEM((2, chips * CORES * cap, d_expert), BF16),
                pltpu.VMEM((num_devices, top_k, LANES), F32),
                pltpu.VMEM((chips, num_experts, LANES), F32),
                pltpu.VMEM((chips, num_experts, LANES), F32),
                pltpu.VMEM((2, 2, side, CORES, local_experts, side, CORES * cap, piece), BF16),
                pltpu.VMEM((2, 2, side, CORES, num_tokens, piece), F32),
                pltpu.VMEM((2, 2, side, CORES, num_tokens, piece), F32),
                dma, dma, dma, dma((2, local_experts)), dma, dma, dma((2,)), dma((side, side)), dma((side, side)),
                dma((2,)), dma((2, 2, side)), dma((2,)), dma((2, 2, 2)),
            ],
            compiler_params=pltpu.CompilerParams(collective_id=0, has_side_effects=True, vmem_limit_bytes=67043328),
        )(tokens, routes.T, w_router, w_one, w_three, w_two)

    return jax.shard_map(device_step, mesh=mesh, in_specs=(row_spec, row_spec, P(None, None), expert_spec, expert_spec, expert_spec), out_specs=row_spec, check_vma=False)
```

time: 85.2 us -> 78.5 us (0.921)
  Pallas kernels: 83.3 us -> 76.7 us
    pallas_call x1, Pallas kernels: 83.3 us -> 76.7 us  [device_step(): pl.pallas_call(functools.partial(moe_kernel, side), out_shape=jax.ShapeDt...]
where the time goes in v3:
time: 78.5 us; the launch traced here: 78.4 us
  Pallas kernels  76.7 us (98%)
  local copies, waits for them, and re-layouts  1.67 us (2%)
    pallas_call x1, Pallas kernels, device_step(): pl.pallas_call(functools.partial(moe_kernel, side), out_shape=jax.ShapeDt...  76.7 us
    unnamed x1, local copies, waits for them, and re-layouts  1.67 us

profile of v3, /device:TPU:97, one launch (start us, length us, event | category | flops | bytes accessed | tf_op | source)
XLA Modules:
  0.0 78.4 jit_solution(10168843792597380527)
XLA Ops:
  0.0 76.7 %shard_map.64 = bf16[64,2048]{1,0:T(8,128)(2,1)} custom-call(bf16[64,2048]{1,0:T(8,128)(2,1)} %x_hbm.1, s32[8,64]{1,0:T(8,128)} %bitcast.1, bf16[2048,128]{1,0:T(8,128)(2,1)} %wr_hbm.1, bf16[4,2048,768]{2,1,0:T(8,128)(2,1)} %w1_hbm.1, bf16[4,2048,768]{2,1,0:T(8,128)(2,1)} %w3_hbm.1, bf16[4,768,2048]{2,1,0:T(8,128)(2,1)} %w2_hbm.1), custom_call_target="tpu_custom_call" | custom-call | tf_op jit(solution)/shard_map/pallas_call | solution.py:483
  76.7 1.7 %copy.8 = bf16[64,2048]{1,0:T(8,128)(2,1)} copy(bf16[64,2048]{1,0:T(8,128)(2,1)} %shard_map.64) | data formatting | bytes 524288

commit v4 on v3

--- a/solution.py
+++ b/solution.py
@@ -22,9 +22,9 @@
 def moe_kernel(
     side,
     x_hbm, routes_hbm, wr_hbm, w1_hbm, w3_hbm, w2_hbm, y_ref,
-    xg, routes_ref, wr, w13, w2, xo, hid, meta, slots, gates, mbuf, pbuf, ybuf,
+    xg, routes_ref, wr, w13, w2, xo, hid, meta, slots, gates, mbuf, pbuf, rbuf, ybuf,
     x_sem, wr_sem, routes_sem, w_sem, meta_ssem, meta_rsem, ag_ssem, ag_rsem, core_rsem,
-    r1_ssem, r1_rsem, r2_ssem, r2_rsem,
+    r1_ssem, r1_rsem, relay_ssem, relay_rsem, r2_ssem, r2_rsem,
 ):
     num_devices = CORES * side * side
     chips = side * side
@@ -94,6 +94,54 @@
 
 
     pltpu.make_async_copy(xg.at[:, me], xg.at[:, me], x_sem).wait()
+
+    pl.semaphore_wait(barrier, num_devices - 1)
+
+    def place(h, a, b):
+        if h == 0:
+            return ring(my_y, b), ring(my_x, a)
+        return ring(my_y, a), ring(my_x, b)
+
+    def block_src(h, a, b, c):
+        y, x = place(h, a, b)
+        return dev(y, x, c)
+
+    def move_block(h, src, rsem, target):
+        return remote(xg.at[h, src], xg.at[h, src], ag_ssem.at[h], rsem, target)
+
+    def first_copy(h, k):
+        return move_block(h, me, ag_rsem.at[side - k, 0], block_src(h, k, 0, core))
+
+    def first_relay(h):
+        k = 1 + core * (side - 2)
+        return move_block(h, block_src(h, k, 0, core), ag_rsem.at[side // 2, 0], block_src(h, side - k, 0, core))
+
+    def second_copy(h, a, k):
+        return move_block(h, block_src(h, a, 0, core), ag_rsem.at[a, side - k], block_src(h, 0, k, core))
+
+    def relay_copy(h, a, k):
+        return move_block(h, block_src(h, a, k, core), ag_rsem.at[a, side // 2], block_src(h, 0, side - k, core))
+
+    def core_copy(h, a, b):
+        return move_block(h, block_src(h, a, b, core), core_rsem.at[a, b], partner)
+
+    def wait_blocks(sem):
+        pltpu.make_async_copy(xg.at[:, me], xg.at[:, me], sem).wait()
+
+    def meta_copy(i):
+        return remote(meta.at[me], meta.at[me], meta_ssem, meta_rsem, lax.rem(me + i, num_devices))
+
+    def send_meta(i, carry):
+        meta_copy(i).start()
+        return carry
+
+    def wait_meta(sem):
+        others = meta.at[pl.ds(0, num_devices - 1)]
+        pltpu.make_async_copy(others, others, sem).wait()
+
+    for h in range(2):
+        for k in (1, side - 1):
+            first_copy(h, k).start()
 
     wr_copy.wait()
     routes_copy.wait()
@@ -110,53 +158,6 @@
     gate = ex / jnp.sum(ex, axis=0, keepdims=True)
     meta[me] = jnp.concatenate([routes.astype(F32) + 1.0, gate], axis=1)
 
-    pl.semaphore_wait(barrier, num_devices - 1)
-
-    def place(h, a, b):
-        if h == 0:
-            return ring(my_y, b), ring(my_x, a)
-        return ring(my_y, a), ring(my_x, b)
-
-    def block_src(h, a, b, c):
-        y, x = place(h, a, b)
-        return dev(y, x, c)
-
-    def move_block(h, src, rsem, target):
-        return remote(xg.at[h, src], xg.at[h, src], ag_ssem.at[h], rsem, target)
-
-    def first_copy(h, k):
-        return move_block(h, me, ag_rsem.at[side - k, 0], block_src(h, k, 0, core))
-
-    def first_relay(h):
-        k = 1 + core * (side - 2)
-        return move_block(h, block_src(h, k, 0, core), ag_rsem.at[side // 2, 0], block_src(h, side - k, 0, core))
-
-    def second_copy(h, a, k):
-        return move_block(h, block_src(h, a, 0, core), ag_rsem.at[a, side - k], block_src(h, 0, k, core))
-
-    def relay_copy(h, a, k):
-        return move_block(h, block_src(h, a, k, core), ag_rsem.at[a, side // 2], block_src(h, 0, side - k, core))
-
-    def core_copy(h, a, b):
-        return move_block(h, block_src(h, a, b, core), core_rsem.at[a, b], partner)
-
-    def wait_blocks(sem):
-        pltpu.make_async_copy(xg.at[:, me], xg.at[:, me], sem).wait()
-
-    def meta_copy(i):
-        return remote(meta.at[me], meta.at[me], meta_ssem, meta_rsem, lax.rem(me + i, num_devices))
-
-    def send_meta(i, carry):
-        meta_copy(i).start()
-        return carry
-
-    def wait_meta(sem):
-        others = meta.at[pl.ds(0, num_devices - 1)]
-        pltpu.make_async_copy(others, others, sem).wait()
-
-    for h in range(2):
-        for k in (1, side - 1):
-            first_copy(h, k).start()
     lax.fori_loop(1, num_devices, send_meta, 0)
     for h in range(2):
         for k in (1, side - 1):
@@ -216,17 +217,12 @@
             for k in (1, side - 1):
                 second_copy(h, a, k).start()
 
-    def next_lines(a, carry):
-        land(a, 1)
-        for h in range(2):
-            relay_copy(h, a, 1).start()
-        land(a + far, side - 1)
-        for h in range(2):
-            relay_copy(h, a + far, side - 1).start()
-        land(a + far, 1)
-        land(a, side - 1)
-        finish(a, 0)
-        finish(a + far, 0)
+    def relay(a, k):
+        for h in range(2):
+            relay_copy(h, a, k).start()
+
+    def own_lines(p, carry):
+        finish(spot(p), 0)
         return carry
 
     def near_lines(p, carry):
@@ -248,8 +244,20 @@
     lax.fori_loop(0, chips, plan_chip, 0)
     land(far, 0)
     same_line(far)
-    lax.fori_loop(0, far, next_lines, 0)
+    land(0, 1)
+    relay(0, 1)
+    land(0, side - 1)
+    land(1, 1)
+    relay(1, 1)
+    land(side - 1, side - 1)
+    relay(side - 1, side - 1)
+    land(1, side - 1)
+    land(side - 1, 1)
+    lax.fori_loop(0, side - 1, own_lines, 0)
     lax.fori_loop(0, side - 1, near_lines, 0)
+    land(far, side - 1)
+    relay(far, side - 1)
+    land(far, 1)
 
     def r1_place(h, k):
         if h == 0:
@@ -309,13 +317,14 @@
 
         def up(t, carry):
             rows = read_rows(part, e)
-            cols = pl.ds(pl.multiple_of(t * n1, n1), n1)
+            cols = pl.ds(t * n1, n1)
             a = jnp.dot(rows, w13[e, 0, :, cols], preferred_element_type=F32)
             b = jnp.dot(rows, w13[e, 1, :, cols], preferred_element_type=F32)
             hid[e % 2, spans[part], cols] = (a * jax.nn.sigmoid(a) * b).astype(BF16)
             return carry
 
-        lax.fori_loop(0, d_expert // n1, up, 0)
+        for t in range(d_expert // n1):
+            up(t, 0)
 
     def send_rows(part, e, g, h):
         for k, span in lines[part][1:]:
@@ -333,7 +342,9 @@
                 write_rows(part, e, cols, jnp.dot(hid[e % 2, spans[part], :], w2[e, :, cols], preferred_element_type=F32).astype(BF16))
                 return carry
 
-            lax.fori_loop(0, CORES, down, 0)
+            for c in range(CORES):
+                down(c, 0)
+        for h in range(2):
             send_rows(part, e, g, h)
 
     def wait_down(e):
@@ -344,23 +355,17 @@
             wait_down(e)
 
         def down(t, carry):
-            cols = pl.ds(pl.multiple_of(t * quarter, quarter), quarter)
+            cols = pl.ds(t * quarter, quarter)
             write_rows(part, e, cols, jnp.dot(hid[e % 2, spans[part], :], w2[e, :, cols], preferred_element_type=F32).astype(BF16))
             return carry
 
         for h in range(2):
-            lax.fori_loop(h * CORES, (h + 1) * CORES, down, 0)
+            for t in range(h * CORES, (h + 1) * CORES):
+                down(t, 0)
             for g in range(2):
                 send_rows(part, e, g, h)
 
     early = 2
-
-    def near_expert(e, carry):
-        up_rows('near', e)
-        for i in range(far):
-            land(spot(e * far + i), far)
-        down_rows('near', e)
-        return carry
 
     def far_expert(e, carry):
         up_rows('far', e)
@@ -377,7 +382,15 @@
         down_group('all', e, 1)
         return carry
 
-    lax.fori_loop(0, early, near_expert, 0)
+    for e in range(early):
+        up_rows('near', e)
+        if e > 0:
+            for p in range((e - 1) * far, e * far):
+                land(spot(p), far)
+        down_rows('near', e)
+    for p in range((early - 1) * far, side):
+        land(spot(p), far)
+    finish(far, 0)
     finish(far, 1)
     finish(far, side - 1)
     lax.fori_loop(0, side, far_lines, 0)
@@ -390,9 +403,19 @@
             return my_y, ring(my_x, k)
         return ring(my_y, k), my_x
 
+    via = 1 + core * (side - 2)
+    direct = side - via
+
+    def sum_place(k):
+        return lax.div(k + 1, 2)
+
+    def relay_sums(g, h):
+        y, x = r2_place(h, via)
+        return remote(pbuf.at[g, h, far], rbuf.at[g, h], relay_ssem, relay_rsem.at[g, h], dev(y, x, core))
+
     def r2_copy(g, h, k, cd):
         y, x = r2_place(h, k)
-        return remote(pbuf.at[g, h, k, cd], ybuf.at[g, h, k, core], r2_ssem.at[0], r2_rsem.at[g, h, 0], dev(y, x, cd))
+        return remote(pbuf.at[g, h, k, cd], ybuf.at[g, h, sum_place(k), core], r2_ssem.at[0], r2_rsem.at[g, h, 0], dev(y, x, cd))
 
     def r2_partner(g, h):
         return remote(pbuf.at[g, h, 0, 1 - core], ybuf.at[g, h, 0, core], r2_ssem.at[1], r2_rsem.at[g, h, 1], partner)
@@ -420,21 +443,33 @@
     def wait_bytes(ref, sem):
         pltpu.make_async_copy(ref, ref, sem).wait()
 
+    def pass_on(g):
+        for h in range(2):
+            wait_bytes(rbuf.at[g, h], relay_rsem.at[g, h])
+            pbuf[g, h, via] = pbuf[g, h, via] + rbuf[g, h]
+            for cd in range(CORES):
+                r2_copy(g, h, via, cd).start()
+
     def merge_group(g, carry):
         for h in range(2):
             for k in range(1, side):
                 wait_bytes(mbuf.at[g, h, k], r1_rsem.at[g, h, k])
             wait_bytes(mbuf.at[g, h, 0, 1 - core], r1_rsem.at[g, h, 0])
 
-        def merge_remote(i, c2):
-            k = lax.rem(i + 1, side - 1) + 1
-            for h in range(2):
-                merge(g, h, k)
-                for cd in range(CORES):
-                    r2_copy(g, h, k, cd).start()
-            return c2
-
-        lax.fori_loop(0, side - 1, merge_remote, 0)
+        for h in range(2):
+            merge(g, h, far)
+            relay_sums(g, h).start()
+
+        @pl.when(g > 0)
+        def _():
+            pass_on(g - 1)
+
+        for h in range(2):
+            merge(g, h, direct)
+            for cd in range(CORES):
+                r2_copy(g, h, direct, cd).start()
+        for h in range(2):
+            merge(g, h, via)
         for h in range(2):
             merge(g, h, 0)
             r2_partner(g, h).start()
@@ -442,14 +477,15 @@
         return carry
 
     lax.fori_loop(0, 2, merge_group, 0)
+    pass_on(1)
 
     for g in range(2):
         for h in range(2):
-            wait_bytes(ybuf.at[g, h, pl.ds(1, side - 1)], r2_rsem.at[g, h, 0])
+            wait_bytes(ybuf.at[g, h, pl.ds(1, 2)], r2_rsem.at[g, h, 0])
             wait_bytes(ybuf.at[g, h, 0, 1 - core], r2_rsem.at[g, h, 1])
             for c in range(CORES):
                 total = ybuf[g, h, 0, c]
-                for k in range(1, side):
+                for k in range(1, 3):
                     total = total + ybuf[g, h, k, c]
                 y_ref[:, cols_of(g, h, c)] = total.astype(BF16)
 
@@ -458,7 +494,8 @@
         wait_bytes(xg.at[h, pl.ds(0, side - 1 + 2 * side + side + chips)], ag_ssem.at[h])
     wait_bytes(mbuf.at[:, :, pl.ds(1, side - 1)], r1_ssem.at[0])
     wait_bytes(mbuf.at[:, :, 0, 0], r1_ssem.at[1])
-    wait_bytes(pbuf.at[:, :, pl.ds(1, side - 1)], r2_ssem.at[0])
+    wait_bytes(pbuf.at[:, :, pl.ds(0, 2)], r2_ssem.at[0])
+    wait_bytes(rbuf, relay_ssem)
     wait_bytes(pbuf.at[:, :, 0, 0], r2_ssem.at[1])
 
 
@@ -498,9 +535,10 @@
                 pltpu.VMEM((chips, num_experts, LANES), F32),
                 pltpu.VMEM((2, 2, side, CORES, local_experts, side, CORES * cap, piece), BF16),
                 pltpu.VMEM((2, 2, side, CORES, num_tokens, piece), F32),
-                pltpu.VMEM((2, 2, side, CORES, num_tokens, piece), F32),
+                pltpu.VMEM((2, 2, CORES, num_tokens, piece), F32),
+                pltpu.VMEM((2, 2, 3, CORES, num_tokens, piece), F32),
                 dma, dma, dma, dma((2, local_experts)), dma, dma, dma((2,)), dma((side, side)), dma((side, side)),
-                dma((2,)), dma((2, 2, side)), dma((2,)), dma((2, 2, 2)),
+                dma((2,)), dma((2, 2, side)), dma, dma((2, 2)), dma((2,)), dma((2, 2, 2)),
             ],
             compiler_params=pltpu.CompilerParams(collective_id=0, has_side_effects=True, vmem_limit_bytes=67043328),
         )(tokens, routes.T, w_router, w_one, w_three, w_two)

time: 78.5 us -> 72.4 us (0.922)
  Pallas kernels: 76.7 us -> 70.7 us
    pallas_call x1, Pallas kernels: 76.7 us -> 70.7 us  [device_step(): pl.pallas_call(functools.partial(moe_kernel, side), out_shape=jax.ShapeDt...]
where the time goes in v4:
time: 72.4 us; the launch traced here: 72.3 us
  Pallas kernels  70.7 us (98%)
  local copies, waits for them, and re-layouts  1.67 us (2%)
    pallas_call x1, Pallas kernels, device_step(): pl.pallas_call(functools.partial(moe_kernel, side), out_shape=jax.ShapeDt...  70.7 us
    unnamed x1, local copies, waits for them, and re-layouts  1.67 us

profile of v4, /device:TPU:97, one launch (start us, length us, event | category | flops | bytes accessed | tf_op | source)
XLA Modules:
  0.0 72.3 jit_solution(10623790772926803608)
XLA Ops:
  0.0 70.7 %shard_map.64 = bf16[64,2048]{1,0:T(8,128)(2,1)} custom-call(bf16[64,2048]{1,0:T(8,128)(2,1)} %x_hbm.1, s32[8,64]{1,0:T(8,128)} %bitcast.1, bf16[2048,128]{1,0:T(8,128)(2,1)} %wr_hbm.1, bf16[4,2048,768]{2,1,0:T(8,128)(2,1)} %w1_hbm.1, bf16[4,2048,768]{2,1,0:T(8,128)(2,1)} %w3_hbm.1, bf16[4,768,2048]{2,1,0:T(8,128)(2,1)} %w2_hbm.1), custom_call_target="tpu_custom_call" | custom-call | tf_op jit(solution)/shard_map/pallas_call | solution.py:520
  70.7 1.7 %copy.8 = bf16[64,2048]{1,0:T(8,128)(2,1)} copy(bf16[64,2048]{1,0:T(8,128)(2,1)} %shard_map.64) | data formatting | bytes 524288

commit v5 on v4

--- a/solution.py
+++ b/solution.py
@@ -22,7 +22,7 @@
 def moe_kernel(
     side,
     x_hbm, routes_hbm, wr_hbm, w1_hbm, w3_hbm, w2_hbm, y_ref,
-    xg, routes_ref, wr, w13, w2, xo, hid, meta, slots, gates, mbuf, pbuf, rbuf, ybuf,
+    xg, routes_ref, wr, w13, w2, xo, hid, meta, mine, slots, gates, mbuf, pbuf, rbuf, ybuf,
     x_sem, wr_sem, routes_sem, w_sem, meta_ssem, meta_rsem, ag_ssem, ag_rsem, core_rsem,
     r1_ssem, r1_rsem, relay_ssem, relay_rsem, r2_ssem, r2_rsem,
 ):
@@ -64,11 +64,12 @@
 
     barrier = pltpu.get_barrier_semaphore()
 
-    def greet(i, carry):
-        pl.semaphore_signal(barrier, inc=1, device_id={'ep': lax.rem(me + i, num_devices)}, device_id_type=MESH)
-        return carry
-
-    lax.fori_loop(1, num_devices, greet, 0)
+    peers = [partner]
+    for k in range(1, side):
+        for c in range(CORES):
+            peers += [dev(my_y, ring(my_x, k), c), dev(ring(my_y, k), my_x, c)]
+    for peer in peers:
+        pl.semaphore_signal(barrier, inc=1, device_id={'ep': peer}, device_id_type=MESH)
 
     x_copies = [pltpu.make_async_copy(x_hbm.at[:, pl.ds(h * half, half)], xg.at[h, me], x_sem) for h in range(2)]
     for cp in x_copies:
@@ -95,7 +96,7 @@
 
     pltpu.make_async_copy(xg.at[:, me], xg.at[:, me], x_sem).wait()
 
-    pl.semaphore_wait(barrier, num_devices - 1)
+    pl.semaphore_wait(barrier, len(peers))
 
     def place(h, a, b):
         if h == 0:
@@ -128,16 +129,14 @@
     def wait_blocks(sem):
         pltpu.make_async_copy(xg.at[:, me], xg.at[:, me], sem).wait()
 
-    def meta_copy(i):
-        return remote(meta.at[me], meta.at[me], meta_ssem, meta_rsem, lax.rem(me + i, num_devices))
-
-    def send_meta(i, carry):
-        meta_copy(i).start()
-        return carry
-
-    def wait_meta(sem):
-        others = meta.at[pl.ds(0, num_devices - 1)]
-        pltpu.make_async_copy(others, others, sem).wait()
+    def meta_copy(stage, k):
+        ref = (meta.at[my_y, my_x, core], meta.at[my_y, :, core], meta.at[:, :, core])[stage]
+        target = (dev(my_y, ring(my_x, k), core), dev(ring(my_y, k), my_x, core), partner)[stage]
+        return remote(ref, ref, meta_ssem.at[stage], meta_rsem.at[stage], target)
+
+    def wait_meta(stage, sem):
+        ref = (meta.at[0, pl.ds(0, side - 1), 0], meta.at[pl.ds(0, side - 1), :, 0], meta.at[:, :, 0])[stage]
+        pltpu.make_async_copy(ref, ref, sem.at[stage]).wait()
 
     for h in range(2):
         for k in (1, side - 1):
@@ -156,9 +155,10 @@
         [jnp.sum(jnp.where(expert_iota == routes[j:j + 1, :], logits, 0.0), axis=0, keepdims=True) for j in range(top_k)], axis=0)
     ex = jnp.exp(picked - jnp.max(picked, axis=0, keepdims=True))
     gate = ex / jnp.sum(ex, axis=0, keepdims=True)
-    meta[me] = jnp.concatenate([routes.astype(F32) + 1.0, gate], axis=1)
-
-    lax.fori_loop(1, num_devices, send_meta, 0)
+    meta[my_y, my_x, core] = jnp.concatenate([routes.astype(F32) + 1.0, gate], axis=1)
+
+    for k in range(1, side):
+        meta_copy(0, k).start()
     for h in range(2):
         for k in (1, side - 1):
             second_copy(h, 0, k).start()
@@ -167,25 +167,55 @@
     row_i = lax.broadcasted_iota(jnp.int32, (LANES, LANES), 0)
     col_i = lax.broadcasted_iota(jnp.int32, (LANES, LANES), 1)
     before = jnp.where((row_i < col_i) & (row_i // num_tokens == col_i // num_tokens), 1.0, 0.0).astype(BF16)
-    ids = lax.broadcasted_iota(jnp.int32, (num_experts, LANES), 0).astype(F32) + 1.0
-
-    def plan_chip(p, carry):
-        tiles = [meta[CORES * p + c] for c in range(CORES)]
+    tile_ids = lax.broadcasted_iota(jnp.int32, (chip_experts, LANES), 0) + 1
+
+    def chip_ids(y, x):
+        return (tile_ids + chip_at(y, x) * chip_experts).astype(F32)
+
+    def chip_routes(y, x):
+        tiles = [meta[y, x, c] for c in range(CORES)]
         turned = [pltpu.roll(v, num_tokens, 1) for v in tiles]
         low = lax.broadcasted_iota(jnp.int32, tiles[0].shape, 1) < num_tokens
-        picks = jnp.where(low, tiles[0], turned[1])
-        shares = jnp.where(low, turned[0], tiles[1])
-        mask = jnp.zeros((num_experts, LANES), F32)
-        weight = jnp.zeros((num_experts, LANES), F32)
-        for j in range(top_k):
-            hit = ids == picks[j:j + 1, :]
-            mask = jnp.where(hit, 1.0, mask)
-            weight = jnp.where(hit, shares[j:j + 1, :], weight)
+        return jnp.where(low, tiles[0], turned[1]), jnp.where(low, turned[0], tiles[1])
+
+    def slots_of(mask):
         rank = jnp.dot(mask.astype(BF16), before, preferred_element_type=F32)
-        slots[p] = jnp.where(mask > 0.0, rank, -1.0)
-        gates[p] = weight
-        return carry
-
+        return jnp.where(mask > 0.0, rank, -1.0)
+
+    my_ids = chip_ids(my_y, my_x)
+
+    def plan_gather(y, carry):
+        for x in range(side):
+            picks, _ = chip_routes(y, x)
+            mask = jnp.zeros((chip_experts, LANES), F32)
+            for j in range(top_k):
+                mask = jnp.where(my_ids == picks[j:j + 1, :], 1.0, mask)
+            mine[y, x] = mask
+        return carry
+
+    def plan_merge(k, carry):
+        for h in range(2):
+            ids = jnp.concatenate([chip_ids(*r1_place(h, side - j)) for j in range(side)], axis=0)
+            picks, shares = chip_routes(*r2_place(h, k))
+            mask = jnp.zeros(ids.shape, F32)
+            weight = jnp.zeros(ids.shape, F32)
+            for j in range(top_k):
+                hit = ids == picks[j:j + 1, :]
+                mask = jnp.where(hit, 1.0, mask)
+                weight = jnp.where(hit, shares[j:j + 1, :], weight)
+            slots[h, k] = slots_of(mask)
+            gates[h, k] = weight
+        return carry
+
+    def r1_place(h, k):
+        if h == 0:
+            return ring(my_y, k), my_x
+        return my_y, ring(my_x, k)
+
+    def r2_place(h, k):
+        if h == 0:
+            return my_y, ring(my_x, k)
+        return ring(my_y, k), my_x
 
     pair_row = lax.broadcasted_iota(jnp.int32, (CORES * cap, LANES), 0)
     pair_lane = lax.broadcasted_iota(jnp.int32, (CORES * cap, LANES), 1)
@@ -194,8 +224,8 @@
     def gather_chip(h, a, b):
         p = chip_at(*place(h, a, b))
         py, px = (spot(b), spot(a)) if h == 0 else (spot(a), spot(b))
-        mine = slots[p, pl.ds(me * local_experts, local_experts), :]
-        pick = jnp.where(mine[:, None, :] == wanted[None], 1.0, 0.0).reshape(local_experts * CORES * cap, LANES).astype(BF16)
+        found = mine[place(h, a, b)[0], place(h, a, b)[1], pl.ds(core * local_experts, local_experts), :]
+        pick = jnp.where(found[:, None, :] == wanted[None], 1.0, 0.0).reshape(local_experts * CORES * cap, LANES).astype(BF16)
         rows = xg[h, pl.ds(p * CORES, CORES)].reshape(CORES * num_tokens, half)
         out = jnp.dot(pick, rows, preferred_element_type=F32).astype(BF16)
         xo[:, py, px, :, pl.ds(h * half, half)] = out.reshape(local_experts, CORES * cap, half)
@@ -238,15 +268,22 @@
         land(a, 0)
     for h in range(2):
         first_relay(h).start()
+    wait_meta(0, meta_rsem)
+    for k in range(1, side):
+        meta_copy(1, k).start()
     for a in near[:2]:
         same_line(a)
-    wait_meta(meta_rsem)
-    lax.fori_loop(0, chips, plan_chip, 0)
-    land(far, 0)
-    same_line(far)
     land(0, 1)
     relay(0, 1)
     land(0, side - 1)
+    wait_meta(1, meta_rsem)
+    meta_copy(2, 0).start()
+    land(far, 0)
+    same_line(far)
+    wait_meta(2, meta_rsem)
+    lax.fori_loop(0, side, plan_gather, 0)
+    mine[...] = slots_of(mine[...].reshape(chips * chip_experts, LANES)).reshape(side, side, chip_experts, LANES)
+    lax.fori_loop(0, side, plan_merge, 0)
     land(1, 1)
     relay(1, 1)
     land(side - 1, side - 1)
@@ -257,12 +294,6 @@
     lax.fori_loop(0, side - 1, near_lines, 0)
     land(far, side - 1)
     relay(far, side - 1)
-    land(far, 1)
-
-    def r1_place(h, k):
-        if h == 0:
-            return ring(my_y, k), my_x
-        return my_y, ring(my_x, k)
 
     close, edge = pl.ds(0, side - 1), pl.ds(side - 1, 1)
     whole = pl.ds(0, side)
@@ -303,11 +334,11 @@
     def r1_copy(g, h, e, k, span, cm):
         y, x = r1_place(h, k)
         src = line_ref(h, e, k, span, cols_of(g, h, cm))
-        return remote(src, mbuf.at[g, h, k, core, e, span], r1_ssem.at[0], r1_rsem.at[g, h, k], dev(y, x, cm))
+        return remote(src, mbuf.at[g, h, k, core, e, span], r1_ssem.at[0], r1_rsem.at[g, 0], dev(y, x, cm))
 
     def r1_partner(g, h, e, span):
         src = line_ref(h, e, 0, span, cols_of(g, h, 1 - core))
-        return remote(src, mbuf.at[g, h, 0, core, e, span], r1_ssem.at[1], r1_rsem.at[g, h, 0], partner)
+        return remote(src, mbuf.at[g, h, 0, core, e, span], r1_ssem.at[1], r1_rsem.at[g, 1], partner)
 
     n1 = 256
 
@@ -382,14 +413,15 @@
         down_group('all', e, 1)
         return carry
 
-    for e in range(early):
-        up_rows('near', e)
-        if e > 0:
-            for p in range((e - 1) * far, e * far):
-                land(spot(p), far)
-        down_rows('near', e)
-    for p in range((early - 1) * far, side):
-        land(spot(p), far)
+    up_rows('near', 0)
+    land(far, 1)
+    down_rows('near', 0)
+    land(0, far)
+    up_rows('near', 1)
+    land(1, far)
+    land(side - 1, far)
+    down_rows('near', 1)
+    land(far, far)
     finish(far, 0)
     finish(far, 1)
     finish(far, side - 1)
@@ -398,11 +430,6 @@
     lax.fori_loop(early, local_experts, all_expert, 0)
     lax.fori_loop(early, local_experts, all_second, 0)
 
-    def r2_place(h, k):
-        if h == 0:
-            return my_y, ring(my_x, k)
-        return ring(my_y, k), my_x
-
     via = 1 + core * (side - 2)
     direct = side - via
 
@@ -415,21 +442,18 @@
 
     def r2_copy(g, h, k, cd):
         y, x = r2_place(h, k)
-        return remote(pbuf.at[g, h, k, cd], ybuf.at[g, h, sum_place(k), core], r2_ssem.at[0], r2_rsem.at[g, h, 0], dev(y, x, cd))
+        return remote(pbuf.at[g, h, k, cd], ybuf.at[g, h, sum_place(k), core], r2_ssem.at[0], r2_rsem.at[g, 0], dev(y, x, cd))
 
     def r2_partner(g, h):
-        return remote(pbuf.at[g, h, 0, 1 - core], ybuf.at[g, h, 0, core], r2_ssem.at[1], r2_rsem.at[g, h, 1], partner)
+        return remote(pbuf.at[g, h, 0, 1 - core], ybuf.at[g, h, 0, core], r2_ssem.at[1], r2_rsem.at[g, 1], partner)
 
     def merge(g, h, k):
-        y, x = r2_place(h, k)
-        p = chip_at(y, x)
         q = spot(k)
         lhs = []
         for j in range(side):
-            sy, sx = r1_place(h, side - j)
-            base = pl.multiple_of(chip_at(sy, sx) * chip_experts, chip_experts)
-            hit = slots[p, pl.ds(base, chip_experts), :][:, None, :] == wanted[None]
-            share = gates[p, pl.ds(base, chip_experts), :]
+            span = pl.ds(j * chip_experts, chip_experts)
+            hit = slots[h, k, span, :][:, None, :] == wanted[None]
+            share = gates[h, k, span, :]
             g_hi = share.astype(BF16).astype(F32)
             g_mid = (share - g_hi).astype(BF16).astype(F32)
             g_lo = share - g_hi - g_mid
@@ -451,10 +475,8 @@
                 r2_copy(g, h, via, cd).start()
 
     def merge_group(g, carry):
-        for h in range(2):
-            for k in range(1, side):
-                wait_bytes(mbuf.at[g, h, k], r1_rsem.at[g, h, k])
-            wait_bytes(mbuf.at[g, h, 0, 1 - core], r1_rsem.at[g, h, 0])
+        wait_bytes(mbuf.at[g, :, pl.ds(1, side - 1)], r1_rsem.at[g, 0])
+        wait_bytes(mbuf.at[g, :, 0, 1 - core], r1_rsem.at[g, 1])
 
         for h in range(2):
             merge(g, h, far)
@@ -480,16 +502,17 @@
     pass_on(1)
 
     for g in range(2):
-        for h in range(2):
-            wait_bytes(ybuf.at[g, h, pl.ds(1, 2)], r2_rsem.at[g, h, 0])
-            wait_bytes(ybuf.at[g, h, 0, 1 - core], r2_rsem.at[g, h, 1])
+        wait_bytes(ybuf.at[g, :, pl.ds(1, 2)], r2_rsem.at[g, 0])
+        wait_bytes(ybuf.at[g, :, 0, 1 - core], r2_rsem.at[g, 1])
+        for h in range(2):
             for c in range(CORES):
                 total = ybuf[g, h, 0, c]
                 for k in range(1, 3):
                     total = total + ybuf[g, h, k, c]
                 y_ref[:, cols_of(g, h, c)] = total.astype(BF16)
 
-    wait_meta(meta_ssem)
+    for stage in range(3):
+        wait_meta(stage, meta_ssem)
     for h in range(2):
         wait_bytes(xg.at[h, pl.ds(0, side - 1 + 2 * side + side + chips)], ag_ssem.at[h])
     wait_bytes(mbuf.at[:, :, pl.ds(1, side - 1)], r1_ssem.at[0])
@@ -530,15 +553,16 @@
                 pltpu.VMEM((local_experts, d_expert, d_model), BF16),
                 pltpu.VMEM((local_experts, side, side, CORES * cap, d_model), BF16),
                 pltpu.VMEM((2, chips * CORES * cap, d_expert), BF16),
-                pltpu.VMEM((num_devices, top_k, LANES), F32),
-                pltpu.VMEM((chips, num_experts, LANES), F32),
-                pltpu.VMEM((chips, num_experts, LANES), F32),
+                pltpu.VMEM((side, side, CORES, top_k, LANES), F32),
+                pltpu.VMEM((side, side, CORES * local_experts, LANES), F32),
+                pltpu.VMEM((2, side, side * CORES * local_experts, LANES), F32),
+                pltpu.VMEM((2, side, side * CORES * local_experts, LANES), F32),
                 pltpu.VMEM((2, 2, side, CORES, local_experts, side, CORES * cap, piece), BF16),
                 pltpu.VMEM((2, 2, side, CORES, num_tokens, piece), F32),
                 pltpu.VMEM((2, 2, CORES, num_tokens, piece), F32),
                 pltpu.VMEM((2, 2, 3, CORES, num_tokens, piece), F32),
-                dma, dma, dma, dma((2, local_experts)), dma, dma, dma((2,)), dma((side, side)), dma((side, side)),
-                dma((2,)), dma((2, 2, side)), dma, dma((2, 2)), dma((2,)), dma((2, 2, 2)),
+                dma, dma, dma, dma((2, local_experts)), dma((3,)), dma((3,)), dma((2,)), dma((side, side)), dma((side, side)),
+                dma((2,)), dma((2, 2)), dma, dma((2, 2)), dma((2,)), dma((2, 2)),
             ],
             compiler_params=pltpu.CompilerParams(collective_id=0, has_side_effects=True, vmem_limit_bytes=67043328),
         )(tokens, routes.T, w_router, w_one, w_three, w_two)

time: 72.4 us -> 70.5 us (0.974)
  Pallas kernels: 70.7 us -> 68.7 us
    pallas_call x1, Pallas kernels: 70.7 us -> 68.7 us  [device_step(): pl.pallas_call(functools.partial(moe_kernel, side), out_shape=jax.ShapeDt...]
where the time goes in v5:
time: 70.5 us; the launch traced here: 70.4 us
  Pallas kernels  68.7 us (97%)
  local copies, waits for them, and re-layouts  1.67 us (2%)
    pallas_call x1, Pallas kernels, device_step(): pl.pallas_call(functools.partial(moe_kernel, side), out_shape=jax.ShapeDt...  68.7 us
    unnamed x1, local copies, waits for them, and re-layouts  1.67 us

profile of v5, /device:TPU:97, one launch (start us, length us, event | category | flops | bytes accessed | tf_op | source)
XLA Modules:
  0.0 70.4 jit_solution(14427378720573621874)
XLA Ops:
  0.0 68.7 %shard_map.64 = bf16[64,2048]{1,0:T(8,128)(2,1)} custom-call(bf16[64,2048]{1,0:T(8,128)(2,1)} %x_hbm.1, s32[8,64]{1,0:T(8,128)} %bitcast.1, bf16[2048,128]{1,0:T(8,128)(2,1)} %wr_hbm.1, bf16[4,2048,768]{2,1,0:T(8,128)(2,1)} %w1_hbm.1, bf16[4,2048,768]{2,1,0:T(8,128)(2,1)} %w3_hbm.1, bf16[4,768,2048]{2,1,0:T(8,128)(2,1)} %w2_hbm.1), custom_call_target="tpu_custom_call" | custom-call | tf_op jit(solution)/shard_map/pallas_call | solution.py:543
  68.7 1.7 %copy.8 = bf16[64,2048]{1,0:T(8,128)(2,1)} copy(bf16[64,2048]{1,0:T(8,128)(2,1)} %shard_map.64) | data formatting | bytes 524288

commit v6 on v5

--- a/solution.py
+++ b/solution.py
@@ -124,7 +124,7 @@
         return move_block(h, block_src(h, a, k, core), ag_rsem.at[a, side // 2], block_src(h, 0, side - k, core))
 
     def core_copy(h, a, b):
-        return move_block(h, block_src(h, a, b, core), core_rsem.at[a, b], partner)
+        return move_block(h, block_src(h, a, b, core), core_rsem.at[a, 1 if b == side - 1 else b], partner)
 
     def wait_blocks(sem):
         pltpu.make_async_copy(xg.at[:, me], xg.at[:, me], sem).wait()
@@ -230,15 +230,30 @@
         out = jnp.dot(pick, rows, preferred_element_type=F32).astype(BF16)
         xo[:, py, px, :, pl.ds(h * half, half)] = out.reshape(local_experts, CORES * cap, half)
 
+    def pick_rows(a, b):
+        for h in range(2):
+            gather_chip(h, a, b)
+
     def finish(a, b):
         wait_blocks(core_rsem.at[a, b])
-        for h in range(2):
-            gather_chip(h, a, b)
+        pick_rows(a, b)
+
+    def finish_near(a):
+        four = xg.at[:, pl.ds(0, 2)]
+        pltpu.make_async_copy(four, four, core_rsem.at[a, 1]).wait()
+        pick_rows(a, 1)
+        pick_rows(a, side - 1)
+
+    def arrive(a, b):
+        wait_blocks(ag_rsem.at[a, b])
+
+    def share(a, b):
+        for h in range(2):
+            core_copy(h, a, b).start()
 
     def land(a, b):
-        wait_blocks(ag_rsem.at[a, b])
-        for h in range(2):
-            core_copy(h, a, b).start()
+        arrive(a, b)
+        share(a, b)
 
     near = (1, side - 1) + tuple(range(2, side - 1))
 
@@ -256,8 +271,7 @@
         return carry
 
     def near_lines(p, carry):
-        finish(spot(p), 1)
-        finish(spot(p), side - 1)
+        finish_near(spot(p))
         return carry
 
     def far_lines(p, carry):
@@ -265,7 +279,7 @@
         return carry
 
     for a in near[:2]:
-        land(a, 0)
+        arrive(a, 0)
     for h in range(2):
         first_relay(h).start()
     wait_meta(0, meta_rsem)
@@ -273,27 +287,34 @@
         meta_copy(1, k).start()
     for a in near[:2]:
         same_line(a)
-    land(0, 1)
+    for a in near[:2]:
+        share(a, 0)
+    arrive(0, 1)
     relay(0, 1)
+    share(0, 1)
     land(0, side - 1)
+    arrive(far, 0)
+    same_line(far)
+    share(far, 0)
     wait_meta(1, meta_rsem)
     meta_copy(2, 0).start()
-    land(far, 0)
-    same_line(far)
     wait_meta(2, meta_rsem)
     lax.fori_loop(0, side, plan_gather, 0)
     mine[...] = slots_of(mine[...].reshape(chips * chip_experts, LANES)).reshape(side, side, chip_experts, LANES)
     lax.fori_loop(0, side, plan_merge, 0)
-    land(1, 1)
+    arrive(1, 1)
     relay(1, 1)
-    land(side - 1, side - 1)
+    share(1, 1)
+    arrive(side - 1, side - 1)
     relay(side - 1, side - 1)
+    share(side - 1, side - 1)
     land(1, side - 1)
     land(side - 1, 1)
     lax.fori_loop(0, side - 1, own_lines, 0)
     lax.fori_loop(0, side - 1, near_lines, 0)
-    land(far, side - 1)
+    arrive(far, side - 1)
     relay(far, side - 1)
+    share(far, side - 1)
 
     close, edge = pl.ds(0, side - 1), pl.ds(side - 1, 1)
     whole = pl.ds(0, side)
@@ -423,8 +444,7 @@
     down_rows('near', 1)
     land(far, far)
     finish(far, 0)
-    finish(far, 1)
-    finish(far, side - 1)
+    finish_near(far)
     lax.fori_loop(0, side, far_lines, 0)
     lax.fori_loop(0, early, far_expert, 0)
     lax.fori_loop(early, local_experts, all_expert, 0)
@@ -438,7 +458,7 @@
 
     def relay_sums(g, h):
         y, x = r2_place(h, via)
-        return remote(pbuf.at[g, h, far], rbuf.at[g, h], relay_ssem, relay_rsem.at[g, h], dev(y, x, core))
+        return remote(pbuf.at[g, h, far], rbuf.at[g, h], relay_ssem, relay_rsem.at[g], dev(y, x, core))
 
     def r2_copy(g, h, k, cd):
         y, x = r2_place(h, k)
@@ -468,8 +488,8 @@
         pltpu.make_async_copy(ref, ref, sem).wait()
 
     def pass_on(g):
-        for h in range(2):
-            wait_bytes(rbuf.at[g, h], relay_rsem.at[g, h])
+        wait_bytes(rbuf.at[g], relay_rsem.at[g])
+        for h in range(2):
             pbuf[g, h, via] = pbuf[g, h, via] + rbuf[g, h]
             for cd in range(CORES):
                 r2_copy(g, h, via, cd).start()
@@ -561,8 +581,8 @@
                 pltpu.VMEM((2, 2, side, CORES, num_tokens, piece), F32),
                 pltpu.VMEM((2, 2, CORES, num_tokens, piece), F32),
                 pltpu.VMEM((2, 2, 3, CORES, num_tokens, piece), F32),
-                dma, dma, dma, dma((2, local_experts)), dma((3,)), dma((3,)), dma((2,)), dma((side, side)), dma((side, side)),
-                dma((2,)), dma((2, 2)), dma, dma((2, 2)), dma((2,)), dma((2, 2)),
+                dma, dma, dma, dma((2, local_experts)), dma((3,)), dma((3,)), dma((2,)), dma((side, side)), dma((side, side - 1)),
+                dma((2,)), dma((2, 2)), dma, dma((2,)), dma((2,)), dma((2, 2)),
             ],
             compiler_params=pltpu.CompilerParams(collective_id=0, has_side_effects=True, vmem_limit_bytes=67043328),
         )(tokens, routes.T, w_router, w_one, w_three, w_two)

time: 70.5 us -> 70.4 us (level)
  no operation moved by 1% of the time
where the time goes in v6:
time: 70.4 us; the launch traced here: 70.3 us
  Pallas kernels  68.6 us (97%)
  local copies, waits for them, and re-layouts  1.67 us (2%)
    pallas_call x1, Pallas kernels, device_step(): pl.pallas_call(functools.partial(moe_kernel, side), out_shape=jax.ShapeDt...  68.6 us
    unnamed x1, local copies, waits for them, and re-layouts  1.67 us

profile of v6, /device:TPU:97, one launch (start us, length us, event | category | flops | bytes accessed | tf_op | source)
XLA Modules:
  0.0 70.3 jit_solution(10620128445730624482)
XLA Ops:
  0.0 68.6 %shard_map.64 = bf16[64,2048]{1,0:T(8,128)(2,1)} custom-call(bf16[64,2048]{1,0:T(8,128)(2,1)} %x_hbm.1, s32[8,64]{1,0:T(8,128)} %bitcast.1, bf16[2048,128]{1,0:T(8,128)(2,1)} %wr_hbm.1, bf16[4,2048,768]{2,1,0:T(8,128)(2,1)} %w1_hbm.1, bf16[4,2048,768]{2,1,0:T(8,128)(2,1)} %w3_hbm.1, bf16[4,768,2048]{2,1,0:T(8,128)(2,1)} %w2_hbm.1), custom_call_target="tpu_custom_call" | custom-call | tf_op jit(solution)/shard_map/pallas_call | solution.py:563
  68.6 1.7 %copy.8 = bf16[64,2048]{1,0:T(8,128)(2,1)} copy(bf16[64,2048]{1,0:T(8,128)(2,1)} %shard_map.64) | data formatting | bytes 524288

commit v7 on v6

--- a/solution.py
+++ b/solution.py
@@ -502,14 +502,15 @@
             merge(g, h, far)
             relay_sums(g, h).start()
 
+        for h in range(2):
+            merge(g, h, direct)
+            for cd in range(CORES):
+                r2_copy(g, h, direct, cd).start()
+
         @pl.when(g > 0)
         def _():
             pass_on(g - 1)
 
-        for h in range(2):
-            merge(g, h, direct)
-            for cd in range(CORES):
-                r2_copy(g, h, direct, cd).start()
         for h in range(2):
             merge(g, h, via)
         for h in range(2):

time: 70.4 us -> 70.7 us (level)
  no operation moved by 1% of the time
where the time goes in v7:
time: 70.7 us; the launch traced here: 70.6 us
  Pallas kernels  68.9 us (97%)
  local copies, waits for them, and re-layouts  1.67 us (2%)
    pallas_call x1, Pallas kernels, device_step(): pl.pallas_call(functools.partial(moe_kernel, side), out_shape=jax.ShapeDt...  68.9 us
    unnamed x1, local copies, waits for them, and re-layouts  1.67 us

profile of v7, /device:TPU:97, one launch (start us, length us, event | category | flops | bytes accessed | tf_op | source)
XLA Modules:
  0.0 70.6 jit_solution(8666253483654124914)
XLA Ops:
  0.0 68.9 %shard_map.64 = bf16[64,2048]{1,0:T(8,128)(2,1)} custom-call(bf16[64,2048]{1,0:T(8,128)(2,1)} %x_hbm.1, s32[8,64]{1,0:T(8,128)} %bitcast.1, bf16[2048,128]{1,0:T(8,128)(2,1)} %wr_hbm.1, bf16[4,2048,768]{2,1,0:T(8,128)(2,1)} %w1_hbm.1, bf16[4,2048,768]{2,1,0:T(8,128)(2,1)} %w3_hbm.1, bf16[4,768,2048]{2,1,0:T(8,128)(2,1)} %w2_hbm.1), custom_call_target="tpu_custom_call" | custom-call | tf_op jit(solution)/shard_map/pallas_call | solution.py:564
  68.9 1.7 %copy.8 = bf16[64,2048]{1,0:T(8,128)(2,1)} copy(bf16[64,2048]{1,0:T(8,128)(2,1)} %shard_map.64) | data formatting | bytes 524288
